TPU v7x, 32 devices: a whole 2x2x4 slice. The times are simulated.
32 devices in a mesh: rows: 8 (over y, x, core), cols: 4 (over z).
Axes of the slice: x: 2, y: 2, z: 4, core: 2. Of those that a mesh axis runs over, the one named last changes fastest.
Arguments:
- density: bfloat16 [640, 640], P('rows', 'cols'), as said below
- occupancy: int32 [5, 5], replicated, may hold values from 0 to 1, as said below
- square_filter: int32 [5, 5], replicated, may hold values 0 or 1
- cube_filter: int32 [5, 5], replicated, may hold values 0 or 1
Outputs:
- purified: float32 [640, 640], P('rows', 'cols')
Inputs may be any that keep to these rules, and one draw needn't show every extreme that they name: density is symmetric. occupancy is symmetric and every diagonal tile is stored.
All inputs are finite; a program needn't handle non-finite values.
Results may differ from a plain program's by a relative error of at most 0.0095.
Values may be sent and summed in bfloat16 or wider, within the bound.
No kernel may reach another device: no remote copies, remote signals or barrier semaphores. Data moves between devices by JAX's collectives and lax.ppermute only.
A program may use at most 64 MiB of HBM per device.

v0:
```python
import jax
import jax.numpy as jnp
from jax import lax
from jax.sharding import PartitionSpec as P

TILE = 128


def expand(table, row_start, row_count, col_start, col_count):
    count = table.shape[0]
    tile_ids = jnp.arange(count, dtype=jnp.int32)
    row_tiles = (jnp.arange(row_count, dtype=jnp.int32) + row_start) // TILE
    col_tiles = (jnp.arange(col_count, dtype=jnp.int32) + col_start) // TILE
    row_pick = (row_tiles[:, None] == tile_ids[None, :]).astype(jnp.float32)
    col_pick = (tile_ids[:, None] == col_tiles[None, :]).astype(jnp.float32)
    left = jnp.dot(row_pick, table.astype(jnp.float32), precision=lax.Precision.HIGHEST)
    return jnp.dot(left, col_pick, precision=lax.Precision.HIGHEST)


def over_panel(step, init, occupied):
    return step(init, lax.all_gather(occupied, "rows", axis=0, tiled=True), jnp.int32(0))


def on_device(density, occupancy, square_filter, cube_filter):
    row_count, col_count = density.shape
    row_start = lax.axis_index("rows") * row_count
    col_start = lax.axis_index("cols") * col_count
    stored_mask = expand(occupancy, row_start, row_count, col_start, col_count)
    square_mask = expand(square_filter, row_start, row_count, col_start, col_count)
    cube_mask = expand(cube_filter, row_start, row_count, col_start, col_count)
    occupied = jnp.where(stored_mask > 0.5, density, jnp.zeros_like(density))
    empty = jnp.zeros((row_count, col_count), jnp.float32)
    panel = lax.all_gather(occupied, "cols", axis=1, tiled=True)

    def add_square(total, piece, start):
        return jnp.dot(panel, piece, preferred_element_type=jnp.float32)

    square_total = over_panel(add_square, empty, occupied)
    square = jnp.where(square_mask > 0.5, square_total, 0.0).astype(jnp.bfloat16)
    square_rows = lax.all_gather(square, "cols", axis=1, tiled=True)

    def add_cube(total, piece, start):
        return jnp.dot(square_rows, piece, preferred_element_type=jnp.float32)

    cube_total = over_panel(add_cube, empty, occupied)
    cube = jnp.where(cube_mask > 0.5, cube_total, 0.0)
    return 3.0 * square.astype(jnp.float32) - 2.0 * cube


def solution(mesh):
    placed = (P("rows", "cols"), P(), P(), P())
    return jax.shard_map(
        on_device, mesh=mesh, in_specs=placed, out_specs=P("rows", "cols"), check_vma=False
    )
```

profile of v0, /device:TPU:0, one launch (start us, length us, event | category | flops | bytes accessed | tf_op | source)
XLA Modules:
  0.0 42.6 jit_solution(16775872245500241807)
XLA Ops:
  0.0 0.0 copy-start
  0.0 0.9 %fusion.5 = f32[80,5]{1,0:T(8,128)S(1)} fusion(s32[80]{0:T(128)S(1)} %and_select_fusion.1, s32[5,5]{1,0:T(8,128)} %param.5), kind=kOutput, calls=%fused_computation.11 | convolution fusion | flops 24425 | bytes 2020 | tf_op jit(solution)/shard_map/dot_general | solution.py:16
  0.9 0.0 copy-done
  0.9 0.2 fusion.3
  1.1 0.0 copy-start.1
  1.1 0.1 copy.5
  1.2 0.6 %copy-done.1 = s32[5,5]{1,0:T(8,128)S(1)} copy-done((s32[5,5]{1,0:T(8,128)S(1)}, s32[5,5]{1,0:T(8,128)}, u32[]{:S(2)}) %copy-start.1) | copy-done | bytes 124
  1.8 0.2 fusion.6
  2.0 0.0 copy-start.2
  2.0 0.2 convolution_compare_fusion.2
  2.2 0.5 %copy-done.2 = s32[5,5]{1,0:T(8,128)S(1)} copy-done((s32[5,5]{1,0:T(8,128)S(1)}, s32[5,5]{1,0:T(8,128)}, u32[]{:S(2)}) %copy-start.2) | copy-done | bytes 124
  2.7 0.2 fusion.4
  2.9 0.2 convolution_compare_fusion
  3.1 15.2 %all_gather.10 = bf16[80,640]{0,1:T(8,128)(2,1)S(1)} all-gather(bf16[80,160]{0,1:T(8,128)(2,1)S(1)} %copy.5), channel_id=1, replica_groups=mesh['rows'=8,'cols'=4] {'cols'}, dimensions={1}, use_global_device_ids=true | all-gather | bytes 128000 | tf_op jit(solution)/shard_map/all_gather | solution.py:33
  18.3 9.4 %all_gather.11 = bf16[640,160]{1,0:T(8,128)(2,1)S(1)} all-gather(bf16[80,160]{1,0:T(8,128)(2,1)S(1)} %fusion.3), channel_id=1, replica_groups=mesh['rows'=8,'cols'=4] {'rows'}, dimensions={0}, use_global_device_ids=true | all-gather | bytes 230400 | tf_op jit(solution)/shard_map/all_gather | solution.py:21
  27.7 0.2 fusion.2
  27.9 0.1 copy.6
  28.0 13.7 %all_gather.12 = bf16[80,640]{0,1:T(8,128)(2,1)S(1)} all-gather(bf16[80,160]{0,1:T(8,128)(2,1)S(1)} %copy.6), channel_id=1, replica_groups=mesh['rows'=8,'cols'=4] {'cols'}, dimensions={1}, use_global_device_ids=true | all-gather | bytes 128000 | tf_op jit(solution)/shard_map/all_gather | solution.py:40
  41.7 0.9 %fusion.1 = f32[80,160]{1,0:T(8,128)} fusion(pred[80,160]{1,0:T(8,128)(4,1)S(1)} %convolution_compare_fusion, bf16[80,640]{0,1:T(8,128)(2,1)S(1)} %all_gather.12, bf16[640,160]{1,0:T(8,128)(2,1)S(1)} %all_gather.11, bf16[80,160]{1,0:T(8,128)(2,1)S(1)} %fusion.2), kind=kOutput, calls=%fused_computation.3 | convolution fusion | flops 16448000 | bytes 396800 | tf_op jit(solution)/shard_map/dot_general | solution.py:43
  (2 shorter events, 0.0 us)
Async XLA Ops:
  0.0 0.9 %copy-start = (bf16[80,160]{1,0:T(8,128)(2,1)S(1)}, bf16[80,160]{1,0:T(8,128)(2,1)}, u32[]{:S(2)}) copy-start(bf16[80,160]{1,0:T(8,128)(2,1)} %param.4) | copy-start | bytes 76804
  1.1 0.7 %copy-start.1 = (s32[5,5]{1,0:T(8,128)S(1)}, s32[5,5]{1,0:T(8,128)}, u32[]{:S(2)}) copy-start(s32[5,5]{1,0:T(8,128)} %param.6) | copy-start | bytes 304
  2.0 0.7 %copy-start.2 = (s32[5,5]{1,0:T(8,128)S(1)}, s32[5,5]{1,0:T(8,128)}, u32[]{:S(2)}) copy-start(s32[5,5]{1,0:T(8,128)} %param.7) | copy-start | bytes 304
where the time goes:
time: 42.9 us; the launch traced here: 42.6 us
  blocking collectives  38.3 us (89%)
  matrix products  2.92 us (7%)
  local copies, waits for them, and re-layouts  1.3 us (3%)
    all_gather x1, blocking collectives, on_device(): panel = lax.all_gather(occupied, 'cols', axis=1, tiled=True)  15.2 us
    all_gather x1, blocking collectives, on_device(): square_rows = lax.all_gather(square, 'cols', axis=1, tiled=True)  13.7 us
    all_gather x1, blocking collectives, over_panel(): lax.all_gather(occupied, 'rows', axis=0, tiled=True)  9.43 us
    dot_general x3, matrix products, expand(): jnp.dot(row_pick, table.astype(jnp.float32), precision=lax.Precision.HIGH...  1.33 us
    unnamed x6, local copies, waits for them, and re-layouts  1.08 us
    dot_general x1, matrix products, add_cube(): return jnp.dot(square_rows, piece, preferred_element_type=jnp.float32)  0.86 us

commit v1 on v0

v1 whole, which is shorter than its diff:
```python
import jax
import jax.numpy as jnp
from jax import lax
from jax.sharding import PartitionSpec as P

TILE = 128
SMALL = 4 * 1024 * 1024


def lookup(table, rows, cols):
    tiles = jnp.arange(table.shape[0], dtype=jnp.int32)
    row_pick = (rows[:, None] // TILE == tiles[None, :]).astype(jnp.bfloat16)
    col_pick = (tiles[:, None] == cols[None, :] // TILE).astype(jnp.bfloat16)
    left = jnp.dot(row_pick, table.astype(jnp.bfloat16))
    return jnp.dot(left, col_pick) > 0.5


def span(start, count):
    return jnp.arange(count, dtype=jnp.int32) + start


def gathered(density, occupancy, square_filter, cube_filter):
    b, w = density.shape
    rows = span(lax.axis_index("rows") * b, b)
    cols = span(lax.axis_index("cols") * w, w)
    occupied = jnp.where(lookup(occupancy, rows, cols), density, jnp.zeros_like(density))
    panel = lax.all_gather(occupied, "cols", axis=1, tiled=True)
    column = lax.all_gather(occupied, "rows", axis=0, tiled=True)
    total = jnp.dot(panel, column, preferred_element_type=jnp.float32)
    square = jnp.where(lookup(square_filter, rows, cols), total, 0.0).astype(jnp.bfloat16)
    square_rows = lax.all_gather(square, "cols", axis=1, tiled=True)
    cube = jnp.dot(square_rows, column, preferred_element_type=jnp.float32)
    cube = jnp.where(lookup(cube_filter, rows, cols), cube, 0.0)
    return 3.0 * square.astype(jnp.float32) - 2.0 * cube


def contract_last(a, b):
    return lax.dot_general(a, b, (((1,), (1,)), ((), ())), preferred_element_type=jnp.float32)


def permuted(density, occupancy, square_filter, cube_filter):
    b, w = density.shape
    n_rows, n_cols = lax.axis_size("rows"), lax.axis_size("cols")
    pairs = n_rows // 2
    r, j = lax.axis_index("rows"), lax.axis_index("cols")
    own, parity = r // 2, r % 2

    pieces = [density]
    for s in range(1, n_cols):
        pieces.append(lax.ppermute(density, "cols", [((d + s) % n_cols, d) for d in range(n_cols)]))
    order = jnp.concatenate([span((j + s) % n_cols * w, w) for s in range(n_cols)])
    rows = span(r * b, b)
    stored = lookup(occupancy, rows, order)
    panel = jnp.where(stored, jnp.concatenate(pieces, axis=1), jnp.zeros((), density.dtype))

    other = lax.ppermute(panel, "rows", [(d, d ^ 1) for d in range(n_rows)])
    shifts = sorted(range(1, pairs), key=lambda m: -m)
    panels, groups = [panel], [own]
    for m in shifts:
        panels.append(lax.ppermute(panel, "rows", [((d + 2 * m) % n_rows, d) for d in range(n_rows)]))
        groups.append((own + m) % pairs)
    kept = jnp.concatenate([span((2 * g + parity) * b, b) for g in groups])
    other_rows = span((r ^ 1) * b, b)
    pair_rows = jnp.concatenate([rows, other_rows])
    cols = span(j * w, w)
    square_mask = lookup(square_filter, pair_rows, kept)
    cube_mask = lookup(cube_filter, pair_rows, cols)
    pick = (kept[:, None] == cols[None, :]).astype(jnp.bfloat16)

    right = jnp.concatenate(panels, axis=0)
    left = jnp.concatenate([panel, other], axis=0)
    square = jnp.where(square_mask, contract_last(left, right), 0.0).astype(jnp.bfloat16)
    cube = jnp.dot(square, right[:, :w], preferred_element_type=jnp.float32)
    mine = jnp.dot(square, pick, preferred_element_type=jnp.float32)
    part = 3.0 * mine - 2.0 * jnp.where(cube_mask, cube, 0.0)
    return part[:b] + lax.ppermute(part[b:], "rows", [(d, d ^ 1) for d in range(n_rows)])


def solution(mesh):
    def on_device(density, *tables):
        n_rows, n_cols = mesh.shape["rows"], mesh.shape["cols"]
        small = density.size * n_rows * n_cols * density.dtype.itemsize <= SMALL
        body = permuted if small and n_rows % 2 == 0 else gathered
        return body(density, *tables)

    placed = (P("rows", "cols"), P(), P(), P())
    return jax.shard_map(
        on_device, mesh=mesh, in_specs=placed, out_specs=P("rows", "cols"), check_vma=False
    )
```

time: 42.9 us -> 23 us (0.54)
  blocking collectives: 38.3 us -> 0 us
  starting transfers between devices: 0 us -> 10.7 us
  waiting for transfers between devices: 0 us -> 8.49 us
  matrix products: 2.92 us -> 1.83 us
  other arithmetic: 0.02 us -> 0.96 us
  local copies, waits for them, and re-layouts: 1.3 us -> 0.63 us
    all_gather x3 -> x0, blocking collectives: 38.3 us -> none  [the longest x1 15.2 us: on_device(): panel = lax.all_gather(occupied, 'cols', axis=1, tiled=True)]
    ppermute x0 -> x8, starting transfers between devices: none -> 10.7 us  [the longest x3 6.09 us: permuted(): lax.ppermute(density, 'cols', [((d + s) % n_cols, d) for d in range(n_col...]
    ppermute x0 -> x8, waiting for transfers between devices: none -> 8.49 us  [the longest x3 3.65 us: permuted(): lax.ppermute(density, 'cols', [((d + s) % n_cols, d) for d in range(n_col...]
    dot_general x8 -> x6, matrix products: 2.92 us -> 1.83 us  [the longest x3 1.03 us: lookup(): return jnp.dot(left, col_pick) > 0.5]
    add x0 -> x6, other arithmetic: none -> 0.68 us  [the longest x1 0.65 us: permuted(): part[:b]]
    unnamed x6 -> x8, local copies, waits for them, and re-layouts: 1.08 us -> 0.62 us
  transfers between devices with their start and end apart: 0 -> 8, of which waited for: 0 -> 6; matrix products, arithmetic and copies ran while one was open for 0% -> 4% of each run, Pallas kernels for 0% -> 0%
where the time goes in v1:
time: 23 us; the launch traced here: 22.8 us
  starting transfers between devices  10.7 us (47%)
  waiting for transfers between devices  8.49 us (37%)
  matrix products  1.83 us (8%)
  other arithmetic  0.96 us (4%)
  local copies, waits for them, and re-layouts  0.63 us (3%)
    ppermute x3, starting transfers between devices, permuted(): lax.ppermute(density, 'cols', [((d + s) % n_cols, d) for d in range(n_col...  6.09 us
    ppermute x3, starting transfers between devices, permuted(): lax.ppermute(panel, 'rows', [((d + 2 * m) % n_rows, d) for d in range(n_r...  4.5 us
    ppermute x3, waiting for transfers between devices, permuted(): lax.ppermute(density, 'cols', [((d + s) % n_cols, d) for d in range(n_col...  3.65 us
    ppermute x3, waiting for transfers between devices, permuted(): lax.ppermute(panel, 'rows', [((d + 2 * m) % n_rows, d) for d in range(n_r...  3.57 us
    ppermute x1, waiting for transfers between devices, permuted(): lax.ppermute(part[b:], 'rows', [(d, d ^ 1) for d in range(n_rows)])  1.26 us
    dot_general x3, matrix products, lookup(): return jnp.dot(left, col_pick) > 0.5  1.03 us
    add x1, other arithmetic, permuted(): part[:b]  0.65 us
    unnamed x8, local copies, waits for them, and re-layouts  0.62 us
  transfers between devices with their start and end apart: 8, of which 6 were waited for; matrix products, arithmetic and copies ran while one was open for 4% of the time, Pallas kernels for 0%

profile of v1, /device:TPU:0, one launch (start us, length us, event | category | flops | bytes accessed | tf_op | source)
XLA Modules:
  0.0 22.8 jit_solution(6812025373452127715)
XLA Ops:
  0.0 5.1 %collective-permute-start = (bf16[80,160]{1,0:T(8,128)(2,1)}, bf16[80,160]{1,0:T(8,128)(2,1)S(1)}, u32[]{:S(2)}, u32[]{:S(2)}) collective-permute-start(bf16[80,160]{1,0:T(8,128)(2,1)} %param.4), channel_id=1, source_target_pairs={{1,0},{2,1},{3,2},{0,3},{5,4},{6,5},{7,6},{4,7},{9,8},{10,9},{11,1... | collective-permute-start | bytes 76808 | tf_op jit(solution)/shard_map/ppermute | solution.py:50
  5.1 1.0 %collective-permute-start.2 = (bf16[80,160]{1,0:T(8,128)(2,1)}, bf16[80,160]{1,0:T(8,128)(2,1)S(1)}, u32[]{:S(2)}, u32[]{:S(2)}) collective-permute-start(bf16[80,160]{1,0:T(8,128)(2,1)} %param.4), channel_id=1, source_target_pairs={{3,0},{0,1},{1,2},{2,3},{7,4},{4,5},{5,6},{6,7},{11,8},{8,9},{9,10... | collective-permute-start | bytes 76808 | tf_op jit(solution)/shard_map/ppermute | solution.py:50
  6.2 0.1 and_select_fusion.2
  6.3 0.1 pad_add_fusion.1
  6.3 0.6 %copy-done.1 = s32[5,5]{1,0:T(8,128)S(1)} copy-done((s32[5,5]{1,0:T(8,128)S(1)}, s32[5,5]{1,0:T(8,128)}, u32[]{:S(2)}) %copy-start.1) | copy-done | bytes 124
  7.0 0.4 %convolution_compare_fusion = pred[160,320]{1,0:T(32,128)(4,1)S(1)} fusion(s32[160]{0:T(256)S(1)} %and_select_fusion.2, s32[320]{0:T(512)S(1)} %get-tuple-element.6, s32[5,5]{1,0:T(8,128)S(1)} %copy-done.1), kind=kOutput, calls=%fused_computation.6 | convolution fusion | flops 676025 | bytes 53220 | tf_op jit(solution)/shard_map/dot_general | solution.py:15
  7.3 0.1 add_select_fusion
  7.4 2.7 %collective-permute-done.1 = bf16[80,160]{1,0:T(8,128)(2,1)S(1)} collective-permute-done((bf16[80,160]{1,0:T(8,128)(2,1)}, bf16[80,160]{1,0:T(8,128)(2,1)S(1)}, u32[]{:S(2)}, u32[]{:S(2)}) %collective-permute-start.1) | collective-permute-done | bytes 25632 | tf_op jit(solution)/shard_map/ppermute | solution.py:50
  10.2 0.9 %collective-permute-done.2 = bf16[80,160]{1,0:T(8,128)(2,1)S(1)} collective-permute-done((bf16[80,160]{1,0:T(8,128)(2,1)}, bf16[80,160]{1,0:T(8,128)(2,1)S(1)}, u32[]{:S(2)}, u32[]{:S(2)}) %collective-permute-start.2) | collective-permute-done | bytes 25632 | tf_op jit(solution)/shard_map/ppermute | solution.py:50
  11.1 0.3 %maximum_select_fusion = bf16[80,640]{1,0:T(8,128)(2,1)S(1)} fusion(bf16[80,160]{1,0:T(8,128)(2,1)S(1)} %collective-permute-done.2, bf16[80,160]{1,0:T(8,128)(2,1)S(1)} %collective-permute-done.1, bf16[80,160]{1,0:T(8,128)(2,1)S(1)} %collective-permute-done, bf16[80,160]{1,0:T(8,128)(2,1)S(1)} %copy-done, s32[80]{0:T(128)S(1)} %and_select_fusion.1, ...), kind=kOutput, calls=%fused_computation.32 | convolution fusion | flops 1134025 | bytes 207780 | tf_op jit(solution)/shard_map/dot_general | solution.py:15
  11.4 0.1 collective-permute-start.3
  11.5 1.5 %collective-permute-start.4 = (bf16[80,640]{1,0:T(8,128)(2,1)S(1)}, bf16[80,640]{1,0:T(8,128)(2,1)S(1)}, u32[]{:S(2)}, u32[]{:S(2)}) collective-permute-start(bf16[80,640]{1,0:T(8,128)(2,1)S(1)} %maximum_select_fusion), channel_id=1, source_target_pairs={{24,0},{28,4},{0,8},{4,12},{8,16},{12,20},{16,24},{20,28},{25,1},{... | collective-permute-start | bytes 307208 | tf_op jit(solution)/shard_map/ppermute | solution.py:60
  13.1 1.5 %collective-permute-start.5 = (bf16[80,640]{1,0:T(8,128)(2,1)S(1)}, bf16[80,640]{1,0:T(8,128)(2,1)S(1)}, u32[]{:S(2)}, u32[]{:S(2)}) collective-permute-start(bf16[80,640]{1,0:T(8,128)(2,1)S(1)} %maximum_select_fusion), channel_id=1, source_target_pairs={{16,0},{20,4},{24,8},{28,12},{0,16},{4,20},{8,24},{12,28},{17,1},{... | collective-permute-start | bytes 307208 | tf_op jit(solution)/shard_map/ppermute | solution.py:60
  14.6 1.4 %collective-permute-start.6 = (bf16[80,640]{1,0:T(8,128)(2,1)S(1)}, bf16[80,640]{1,0:T(8,128)(2,1)S(1)}, u32[]{:S(2)}, u32[]{:S(2)}) collective-permute-start(bf16[80,640]{1,0:T(8,128)(2,1)S(1)} %maximum_select_fusion), channel_id=1, source_target_pairs={{8,0},{12,4},{16,8},{20,12},{24,16},{28,20},{0,24},{4,28},{9,1},{1... | collective-permute-start | bytes 307208 | tf_op jit(solution)/shard_map/ppermute | solution.py:60
  16.0 0.3 %convolution_compare_fusion.2 = pred[160,160]{1,0:T(32,128)(4,1)S(1)} fusion(s32[160]{0:T(256)S(1)} %and_select_fusion.2, s32[160]{0:T(256)S(1)} %get-tuple-element.17, s32[5,5]{1,0:T(8,128)S(1)} %copy-done.3), kind=kOutput, calls=%fused_computation.8 | convolution fusion | flops 342425 | bytes 26980 | tf_op jit(solution)/shard_map/dot_general | solution.py:15
  16.4 1.8 %collective-permute-done.4 = bf16[80,640]{1,0:T(8,128)(2,1)S(1)} collective-permute-done((bf16[80,640]{1,0:T(8,128)(2,1)S(1)}, bf16[80,640]{1,0:T(8,128)(2,1)S(1)}, u32[]{:S(2)}, u32[]{:S(2)}) %collective-permute-start.4) | collective-permute-done | bytes 102432 | tf_op jit(solution)/shard_map/ppermute | solution.py:60
  18.2 1.7 %collective-permute-done.5 = bf16[80,640]{1,0:T(8,128)(2,1)S(1)} collective-permute-done((bf16[80,640]{1,0:T(8,128)(2,1)S(1)}, bf16[80,640]{1,0:T(8,128)(2,1)S(1)}, u32[]{:S(2)}, u32[]{:S(2)}) %collective-permute-start.5) | collective-permute-done | bytes 102432 | tf_op jit(solution)/shard_map/ppermute | solution.py:60
  19.9 0.1 collective-permute-done.6
  20.0 0.3 %fusion = bf16[160,320]{1,0:T(8,128)(2,1)S(1)} fusion(pred[160,320]{1,0:T(32,128)(4,1)S(1)} %convolution_compare_fusion, bf16[80,640]{1,0:T(8,128)(2,1)S(1)} %collective-permute-done.6, bf16[80,640]{1,0:T(8,128)(2,1)S(1)} %collective-permute-done.5, bf16[80,640]{1,0:T(8,128)(2,1)S(1)} %collective-permute-done.4, bf16[80,640]{1,0:T(8,128)(2,1)S(1)} %maximum_select_fusion, ...), kind=kOutput, calls=%fused_computation.1 | convolution fusion | flops 67686400 | bytes 665600 | tf_op jit(solution)/shard_map/dot_general | solution.py:38
  20.3 0.3 %convolution_multiply_fusion = f32[160,160]{1,0:T(8,128)S(1)} fusion(bf16[160,320]{1,0:T(8,128)(2,1)S(1)} %fusion, s32[160]{0:T(256)S(1)} %get-tuple-element.18, s32[320]{0:T(512)S(1)} %get-tuple-element.5), kind=kOutput, calls=%fused_computation.5 | convolution fusion | flops 16460800 | bytes 206720 | tf_op jit(solution)/shard_map/dot_general | solution.py:74
  20.6 0.2 fusion.2
  20.8 0.1 collective-permute-start.7
  20.9 1.3 %collective-permute-done.7 = f32[80,160]{1,0:T(8,128)S(1)} collective-permute-done((f32[80,160]{1,0:T(8,128)S(1)}, f32[80,160]{1,0:T(8,128)S(1)}, u32[]{:S(2)}, u32[]{:S(2)}) %collective-permute-start.7) | collective-permute-done | bytes 51232 | tf_op jit(solution)/shard_map/ppermute | solution.py:76
  22.1 0.6 %slice_add_fusion = f32[80,160]{1,0:T(8,128)} fusion(f32[80,160]{1,0:T(8,128)S(1)} %collective-permute-done.7, f32[160,160]{1,0:T(8,128)S(1)} %fusion.2), kind=kLoop, calls=%fused_computation.33 | loop fusion | flops 12800 | bytes 153600 | tf_op jit(solution)/shard_map/add | solution.py:76
  (18 shorter events, 0.1 us)
Async XLA Ops:
  0.0 7.4 %collective-permute-start = (bf16[80,160]{1,0:T(8,128)(2,1)}, bf16[80,160]{1,0:T(8,128)(2,1)S(1)}, u32[]{:S(2)}, u32[]{:S(2)}) collective-permute-start(bf16[80,160]{1,0:T(8,128)(2,1)} %param.4), channel_id=1, source_target_pairs={{1,0},{2,1},{3,2},{0,3},{5,4},{6,5},{7,6},{4,7},{9,8},{10,9},{11,1... | collective-permute-start | bytes 76808 | tf_op jit(solution)/shard_map/ppermute | solution.py:50
  5.1 5.1 %collective-permute-start.1 = (bf16[80,160]{1,0:T(8,128)(2,1)}, bf16[80,160]{1,0:T(8,128)(2,1)S(1)}, u32[]{:S(2)}, u32[]{:S(2)}) collective-permute-start(bf16[80,160]{1,0:T(8,128)(2,1)} %param.4), channel_id=1, source_target_pairs={{2,0},{3,1},{0,2},{1,3},{6,4},{7,5},{4,6},{5,7},{10,8},{11,9},{8,1... | collective-permute-start | bytes 76808 | tf_op jit(solution)/shard_map/ppermute | solution.py:50
  5.1 6.0 %collective-permute-start.2 = (bf16[80,160]{1,0:T(8,128)(2,1)}, bf16[80,160]{1,0:T(8,128)(2,1)S(1)}, u32[]{:S(2)}, u32[]{:S(2)}) collective-permute-start(bf16[80,160]{1,0:T(8,128)(2,1)} %param.4), channel_id=1, source_target_pairs={{3,0},{0,1},{1,2},{2,3},{7,4},{4,5},{5,6},{6,7},{11,8},{8,9},{9,10... | collective-permute-start | bytes 76808 | tf_op jit(solution)/shard_map/ppermute | solution.py:50
  6.3 0.7 %copy-start.1 = (s32[5,5]{1,0:T(8,128)S(1)}, s32[5,5]{1,0:T(8,128)}, u32[]{:S(2)}) copy-start(s32[5,5]{1,0:T(8,128)} %param.6) | copy-start | bytes 304
  7.0 4.1 %copy-start = (bf16[80,160]{1,0:T(8,128)(2,1)S(1)}, bf16[80,160]{1,0:T(8,128)(2,1)}, u32[]{:S(2)}) copy-start(bf16[80,160]{1,0:T(8,128)(2,1)} %param.4) | copy-start | bytes 76804
  7.3 3.8 %copy-start.2 = (s32[5,5]{1,0:T(8,128)S(1)}, s32[5,5]{1,0:T(8,128)}, u32[]{:S(2)}) copy-start(s32[5,5]{1,0:T(8,128)} %param.5) | copy-start | bytes 304
  7.4 8.6 %copy-start.3 = (s32[5,5]{1,0:T(8,128)S(1)}, s32[5,5]{1,0:T(8,128)}, u32[]{:S(2)}) copy-start(s32[5,5]{1,0:T(8,128)} %param.7) | copy-start | bytes 304
  11.4 4.9 %collective-permute-start.3 = (bf16[80,640]{1,0:T(8,128)(2,1)S(1)}, bf16[80,640]{1,0:T(8,128)(2,1)S(1)}, u32[]{:S(2)}, u32[]{:S(2)}) collective-permute-start(bf16[80,640]{1,0:T(8,128)(2,1)S(1)} %maximum_select_fusion), channel_id=1, source_target_pairs={{0,4},{4,0},{8,12},{12,8},{16,20},{20,16},{24,28},{28,24},{1,5},{5... | collective-permute-start | bytes 307208 | tf_op jit(solution)/shard_map/ppermute | solution.py:56
  11.5 6.7 %collective-permute-start.4 = (bf16[80,640]{1,0:T(8,128)(2,1)S(1)}, bf16[80,640]{1,0:T(8,128)(2,1)S(1)}, u32[]{:S(2)}, u32[]{:S(2)}) collective-permute-start(bf16[80,640]{1,0:T(8,128)(2,1)S(1)} %maximum_select_fusion), channel_id=1, source_target_pairs={{24,0},{28,4},{0,8},{4,12},{8,16},{12,20},{16,24},{20,28},{25,1},{... | collective-permute-start | bytes 307208 | tf_op jit(solution)/shard_map/ppermute | solution.py:60
  13.1 6.8 %collective-permute-start.5 = (bf16[80,640]{1,0:T(8,128)(2,1)S(1)}, bf16[80,640]{1,0:T(8,128)(2,1)S(1)}, u32[]{:S(2)}, u32[]{:S(2)}) collective-permute-start(bf16[80,640]{1,0:T(8,128)(2,1)S(1)} %maximum_select_fusion), channel_id=1, source_target_pairs={{16,0},{20,4},{24,8},{28,12},{0,16},{4,20},{8,24},{12,28},{17,1},{... | collective-permute-start | bytes 307208 | tf_op jit(solution)/shard_map/ppermute | solution.py:60
  14.6 5.4 %collective-permute-start.6 = (bf16[80,640]{1,0:T(8,128)(2,1)S(1)}, bf16[80,640]{1,0:T(8,128)(2,1)S(1)}, u32[]{:S(2)}, u32[]{:S(2)}) collective-permute-start(bf16[80,640]{1,0:T(8,128)(2,1)S(1)} %maximum_select_fusion), channel_id=1, source_target_pairs={{8,0},{12,4},{16,8},{20,12},{24,16},{28,20},{0,24},{4,28},{9,1},{1... | collective-permute-start | bytes 307208 | tf_op jit(solution)/shard_map/ppermute | solution.py:60
  20.8 1.3 %collective-permute-start.7 = (f32[80,160]{1,0:T(8,128)S(1)}, f32[80,160]{1,0:T(8,128)S(1)}, u32[]{:S(2)}, u32[]{:S(2)}) collective-permute-start(f32[80,160]{1,0:T(8,128)S(1)} %slice.13), channel_id=1, source_target_pairs={{0,4},{4,0},{8,12},{12,8},{16,20},{20,16},{24,28},{28,24},{1,5},{5... | collective-permute-start | bytes 153608 | tf_op jit(solution)/shard_map/ppermute | solution.py:76

commit v2 on v1

v2 whole, which is shorter than its diff:
```python
import jax
import jax.numpy as jnp
from jax import lax
from jax.experimental import pallas as pl
from jax.experimental.pallas import tpu as pltpu
from jax.sharding import PartitionSpec as P


TILE = 128
SMALL = 4 * 1024 * 1024
PARAMS = pltpu.CompilerParams(vmem_limit_bytes=8 * 1024 * 1024)


def lookup(table, rows, cols):
    tiles = jnp.arange(table.shape[0], dtype=jnp.int32)
    row_pick = (rows[:, None] // TILE == tiles[None, :]).astype(jnp.bfloat16)
    col_pick = (tiles[:, None] == cols[None, :] // TILE).astype(jnp.bfloat16)
    left = jnp.dot(row_pick, table.astype(jnp.bfloat16))
    return jnp.dot(left, col_pick)


def span(start, count):
    return jnp.arange(count, dtype=jnp.int32) + start


def gathered(density, occupancy, square_filter, cube_filter):
    b, w = density.shape
    rows = span(lax.axis_index("rows") * b, b)
    cols = span(lax.axis_index("cols") * w, w)
    occupied = density * lookup(occupancy, rows, cols).astype(density.dtype)
    panel = lax.all_gather(occupied, "cols", axis=1, tiled=True)
    column = lax.all_gather(occupied, "rows", axis=0, tiled=True)
    total = jnp.dot(panel, column, preferred_element_type=jnp.float32)
    square = jnp.where(lookup(square_filter, rows, cols) > 0.5, total, 0.0).astype(jnp.bfloat16)
    square_rows = lax.all_gather(square, "cols", axis=1, tiled=True)
    cube = jnp.dot(square_rows, column, preferred_element_type=jnp.float32)
    cube = jnp.where(lookup(cube_filter, rows, cols) > 0.5, cube, 0.0)
    return 3.0 * square.astype(jnp.float32) - 2.0 * cube


def call(kernel, outs, args):
    held = [pltpu.with_memory_space_constraint(x, pltpu.VMEM) for x in args]
    spec = pl.BlockSpec(memory_space=pltpu.VMEM)
    return pl.pallas_call(
        kernel,
        out_shape=outs,
        in_specs=[spec] * len(held),
        out_specs=jax.tree.map(lambda _: spec, outs),
        compiler_params=PARAMS,
    )(*held)


def panel_kernel(*refs):
    pieces, (stored, panel) = refs[:-2], refs[-2:]
    panel[...] = jnp.concatenate([ref[...] for ref in pieces], axis=1) * stored[...]


def part_kernel(*refs):
    panels, (other, keep, cube_keep, pick, mine, yours) = refs[:-6], refs[-6:]
    b, w = mine.shape
    right = jnp.concatenate([ref[...] for ref in panels], axis=0)
    left = jnp.concatenate([panels[0][...], other[...]], axis=0)
    total = lax.dot_general(left, right, (((1,), (1,)), ((), ())), preferred_element_type=jnp.float32)
    square = (total * keep[...]).astype(jnp.bfloat16)
    cube = jnp.dot(square, right[:, :w], preferred_element_type=jnp.float32)
    own = jnp.dot(square, pick[...], preferred_element_type=jnp.float32)
    part = 3.0 * own - 2.0 * cube * cube_keep[...]
    mine[...] = part[:b]
    yours[...] = part[b:]


def turns(n):
    return sorted(range(1, n), key=lambda s: (s == 1, s))


def flips(n_rows):
    far = sorted(range(2, n_rows, 2), key=lambda f: (-f.bit_count(), f))
    return far + [1]


def permuted(density, occupancy, square_filter, cube_filter):
    b, w = density.shape
    n_rows, n = lax.axis_size("rows"), lax.axis_size("cols")
    r, j = lax.axis_index("rows"), lax.axis_index("cols")

    def swap(x, axis, flip):
        return lax.ppermute(x, axis, [(d, d ^ flip) for d in range(lax.axis_size(axis))])

    shifts = turns(n)
    pieces = [density] + [swap(density, "cols", s) for s in shifts]
    order = jnp.concatenate([span((j ^ s) * w, w) for s in [0] + shifts])
    rows = span(r * b, b)
    stored = lookup(occupancy, rows, order).astype(jnp.bfloat16)
    panel = call(panel_kernel, pltpu.VMEM((b, n * w), density.dtype), [*pieces, stored])

    got = {f: swap(panel, "rows", f) for f in flips(n_rows)}
    other = got.pop(1)
    kept = jnp.concatenate([span((r ^ f) * b, b) for f in [0] + list(got)])
    pair = jnp.concatenate([rows, span((r ^ 1) * b, b)])
    cols = span(j * w, w)
    keep = lookup(square_filter, pair, kept)
    cube_keep = lookup(cube_filter, pair, cols)
    pick = (kept[:, None] == cols[None, :]).astype(jnp.bfloat16)
    part = pltpu.VMEM((b, w), jnp.float32)
    args = [panel, *got.values(), other, keep, cube_keep, pick]
    mine, yours = call(part_kernel, [part, part], args)
    return mine + swap(yours, "rows", 1)


def solution(mesh):
    n_rows, n_cols = mesh.shape["rows"], mesh.shape["cols"]

    def on_device(density, *tables):
        powers = all(k & (k - 1) == 0 for k in (n_rows, n_cols))
        small = density.size * n_rows * n_cols * density.dtype.itemsize <= SMALL
        fits = small and powers and n_rows > 1 and density.shape[0] % 16 == 0
        return (permuted if fits else gathered)(density, *tables)

    placed = (P("rows", "cols"), P(), P(), P())
    return jax.shard_map(
        on_device, mesh=mesh, in_specs=placed, out_specs=P("rows", "cols"), check_vma=False
    )
```

time: 23 us -> 21.8 us (0.948)
  starting transfers between devices: 10.7 us -> 9.34 us
  matrix products: 1.83 us -> 1.02 us
  Pallas kernels: 0 us -> 0.65 us
  local copies, waits for them, and re-layouts: 0.63 us -> 0.95 us
    ppermute x8, starting transfers between devices: 10.7 us -> 9.34 us  [swap(): lax.ppermute(x, axis, [(d, d ^ flip) for d in range(lax.axis_size(axis))])]
    dot_general x6 -> x3, matrix products: 1.83 us -> 1.02 us  [lookup(): return jnp.dot(left, col_pick)]
    pallas_call x0 -> x2, Pallas kernels: none -> 0.65 us  [call(): pl.pallas_call(kernel, out_shape=outs, in_specs=[spec] * len(held), out_s...]
    unnamed x8, local copies, waits for them, and re-layouts: 0.62 us -> 0.95 us
  transfers between devices with their start and end apart: 8 -> 8, of which waited for: 6 -> 5; matrix products, arithmetic and copies ran while one was open for 4% -> 7% of each run, Pallas kernels for 0% -> 0%
where the time goes in v2:
time: 21.8 us; the launch traced here: 21.6 us
  starting transfers between devices  9.34 us (43%)
  waiting for transfers between devices  8.43 us (39%)
  other arithmetic  1.06 us (5%)
  matrix products  1.02 us (5%)
  local copies, waits for them, and re-layouts  0.95 us (4%)
  Pallas kernels  0.65 us (3%)
    ppermute x8, starting transfers between devices, swap(): lax.ppermute(x, axis, [(d, d ^ flip) for d in range(lax.axis_size(axis))])  9.34 us
    ppermute x8, waiting for transfers between devices, swap(): lax.ppermute(x, axis, [(d, d ^ flip) for d in range(lax.axis_size(axis))])  8.43 us
    dot_general x3, matrix products, lookup(): return jnp.dot(left, col_pick)  1.02 us
    unnamed x8, local copies, waits for them, and re-layouts  0.95 us
    pallas_call x2, Pallas kernels, call(): pl.pallas_call(kernel, out_shape=outs, in_specs=[spec] * len(held), out_s...  0.65 us
    add x1, other arithmetic, permuted(): return mine + swap(yours, 'rows', 1)  0.65 us
  transfers between devices with their start and end apart: 8, of which 5 were waited for; matrix products, arithmetic and copies ran while one was open for 7% of the time, Pallas kernels for 0%

profile of v2, /device:TPU:0, one launch (start us, length us, event | category | flops | bytes accessed | tf_op | source)
XLA Modules:
  0.0 21.6 jit_solution(14458251650228650064)
XLA Ops:
  0.0 5.1 %collective-permute-start.1 = (bf16[80,160]{1,0:T(8,128)(2,1)}, bf16[80,160]{1,0:T(8,128)(2,1)S(1)}, u32[]{:S(2)}, u32[]{:S(2)}) collective-permute-start(bf16[80,160]{1,0:T(8,128)(2,1)} %refs_0_.1), channel_id=1, source_target_pairs={{0,3},{1,2},{2,1},{3,0},{4,7},{5,6},{6,5},{7,4},{8,11},{9,10},{10,... | collective-permute-start | bytes 76808 | tf_op jit(solution)/shard_map/ppermute | solution.py:87
  5.1 0.6 %collective-permute-start.2 = (bf16[80,160]{1,0:T(8,128)(2,1)}, bf16[80,160]{1,0:T(8,128)(2,1)S(1)}, u32[]{:S(2)}, u32[]{:S(2)}) collective-permute-start(bf16[80,160]{1,0:T(8,128)(2,1)} %refs_0_.1), channel_id=1, source_target_pairs={{0,1},{1,0},{2,3},{3,2},{4,5},{5,4},{6,7},{7,6},{8,9},{9,8},{10,11... | collective-permute-start | bytes 76808 | tf_op jit(solution)/shard_map/ppermute | solution.py:87
  5.7 0.1 and_select_fusion.1
  5.8 0.1 pad_add_fusion.1
  5.9 0.1 compare_convert_fusion.refs_7_
  6.0 0.1 add_select_fusion
  6.1 0.6 %copy-done.1 = s32[5,5]{1,0:T(8,128)S(1)} copy-done((s32[5,5]{1,0:T(8,128)S(1)}, s32[5,5]{1,0:T(8,128)}, u32[]{:S(2)}) %copy-start.1) | copy-done | bytes 124
  6.7 0.3 %fusion.6.refs_4_ = bf16[80,640]{1,0:T(8,128)(2,1)S(1)} fusion(s32[80]{0:T(128)S(1)} %and_select_fusion.2, s32[640]{0:T(1024)S(1)} %add_select_fusion, s32[5,5]{1,0:T(8,128)S(1)} %copy-done.1), kind=kOutput, calls=%fused_computation.4 | convolution fusion | flops 519625 | bytes 105380 | tf_op jit(solution)/shard_map/dot_general | solution.py:19
  7.0 0.3 %copy-done.2 = s32[5,5]{1,0:T(8,128)S(1)} copy-done((s32[5,5]{1,0:T(8,128)S(1)}, s32[5,5]{1,0:T(8,128)}, u32[]{:S(2)}) %copy-start.2) | copy-done | bytes 124
  7.4 0.3 %fusion.refs_5_ = bf16[160,320]{1,0:T(8,128)(2,1)S(1)} fusion(s32[160]{0:T(256)S(1)} %and_select_fusion.1, s32[320]{0:T(512)S(1)} %get-tuple-element.10, s32[5,5]{1,0:T(8,128)S(1)} %copy-done.2), kind=kOutput, calls=%fused_computation | convolution fusion | flops 522425 | bytes 104420 | tf_op jit(solution)/shard_map/dot_general | solution.py:19
  7.8 2.4 %collective-permute-done.refs_1_ = bf16[80,160]{1,0:T(8,128)(2,1)S(1)} collective-permute-done((bf16[80,160]{1,0:T(8,128)(2,1)}, bf16[80,160]{1,0:T(8,128)(2,1)S(1)}, u32[]{:S(2)}, u32[]{:S(2)}) %collective-permute-start) | collective-permute-done | bytes 25632 | tf_op jit(solution)/shard_map/ppermute | solution.py:87
  10.2 0.1 shard_map.46.refs_0_
  10.3 0.1 collective-permute-start.6
  10.4 1.6 %collective-permute-start.5 = (bf16[80,640]{1,0:T(8,128)(2,1)S(1)}, bf16[80,640]{1,0:T(8,128)(2,1)S(1)}, u32[]{:S(2)}, u32[]{:S(2)}) collective-permute-start(bf16[80,640]{1,0:T(8,128)(2,1)S(1)} %shard_map.46.refs_0_), channel_id=1, source_target_pairs={{0,16},{4,20},{8,24},{12,28},{16,0},{20,4},{24,8},{28,12},{1,17},{... | collective-permute-start | bytes 307208 | tf_op jit(solution)/shard_map/ppermute | solution.py:87
  12.0 1.5 %collective-permute-start.4 = (bf16[80,640]{1,0:T(8,128)(2,1)S(1)}, bf16[80,640]{1,0:T(8,128)(2,1)S(1)}, u32[]{:S(2)}, u32[]{:S(2)}) collective-permute-start(bf16[80,640]{1,0:T(8,128)(2,1)S(1)} %shard_map.46.refs_0_), channel_id=1, source_target_pairs={{0,8},{4,12},{8,0},{12,4},{16,24},{20,28},{24,16},{28,20},{1,9},{5... | collective-permute-start | bytes 307208 | tf_op jit(solution)/shard_map/ppermute | solution.py:87
  13.5 0.5 %collective-permute-start.3 = (bf16[80,640]{1,0:T(8,128)(2,1)S(1)}, bf16[80,640]{1,0:T(8,128)(2,1)S(1)}, u32[]{:S(2)}, u32[]{:S(2)}) collective-permute-start(bf16[80,640]{1,0:T(8,128)(2,1)S(1)} %shard_map.46.refs_0_), channel_id=1, source_target_pairs={{0,24},{4,28},{8,16},{12,20},{16,8},{20,12},{24,0},{28,4},{1,25},{... | collective-permute-start | bytes 307208 | tf_op jit(solution)/shard_map/ppermute | solution.py:87
  13.9 0.3 %fusion.3.refs_6_ = bf16[160,160]{1,0:T(8,128)(2,1)S(1)} fusion(s32[160]{0:T(256)S(1)} %and_select_fusion.1, s32[160]{0:T(256)S(1)} %and_select_fusion, s32[5,5]{1,0:T(8,128)S(1)} %copy-done.3), kind=kOutput, calls=%fused_computation.2 | convolution fusion | flops 265625 | bytes 52580 | tf_op jit(solution)/shard_map/dot_general | solution.py:19
  14.3 1.4 %collective-permute-done.5.refs_3_ = bf16[80,640]{1,0:T(8,128)(2,1)S(1)} collective-permute-done((bf16[80,640]{1,0:T(8,128)(2,1)S(1)}, bf16[80,640]{1,0:T(8,128)(2,1)S(1)}, u32[]{:S(2)}, u32[]{:S(2)}) %collective-permute-start.5) | collective-permute-done | bytes 102432 | tf_op jit(solution)/shard_map/ppermute | solution.py:87
  15.7 2.1 %collective-permute-done.4.refs_2_ = bf16[80,640]{1,0:T(8,128)(2,1)S(1)} collective-permute-done((bf16[80,640]{1,0:T(8,128)(2,1)S(1)}, bf16[80,640]{1,0:T(8,128)(2,1)S(1)}, u32[]{:S(2)}, u32[]{:S(2)}) %collective-permute-start.4) | collective-permute-done | bytes 102432 | tf_op jit(solution)/shard_map/ppermute | solution.py:87
  17.7 1.3 %collective-permute-done.3.refs_1_ = bf16[80,640]{1,0:T(8,128)(2,1)S(1)} collective-permute-done((bf16[80,640]{1,0:T(8,128)(2,1)S(1)}, bf16[80,640]{1,0:T(8,128)(2,1)S(1)}, u32[]{:S(2)}, u32[]{:S(2)}) %collective-permute-start.3) | collective-permute-done | bytes 102432 | tf_op jit(solution)/shard_map/ppermute | solution.py:87
  19.0 0.5 %shard_map.47 = (f32[80,160]{1,0:T(8,128)S(1)}, f32[80,160]{1,0:T(8,128)S(1)}) custom-call(bf16[80,640]{1,0:T(8,128)(2,1)S(1)} %shard_map.46.refs_0_, bf16[80,640]{1,0:T(8,128)(2,1)S(1)} %collective-permute-done.3.refs_1_, bf16[80,640]{1,0:T(8,128)(2,1)S(1)} %collective-permute-done.4.refs_2_, bf16[80,640]{1,0:T(8,128)(2,1)S(1)} %collective-permute-done.5.refs_3_, ...), custom_call_target="tpu_custom_call" | custom-call | tf_op jit(solution)/shard_map/pallas_call | solution.py:44
  19.6 0.1 collective-permute-start.7
  19.7 1.3 %collective-permute-done.7 = f32[80,160]{1,0:T(8,128)S(1)} collective-permute-done((f32[80,160]{1,0:T(8,128)S(1)}, f32[80,160]{1,0:T(8,128)S(1)}, u32[]{:S(2)}, u32[]{:S(2)}) %collective-permute-start.7) | collective-permute-done | bytes 51232 | tf_op jit(solution)/shard_map/ppermute | solution.py:87
  20.9 0.6 %add.170 = f32[80,160]{1,0:T(8,128)} add(f32[80,160]{1,0:T(8,128)S(1)} %get-tuple-element.7, f32[80,160]{1,0:T(8,128)S(1)} %collective-permute-done.7) | non-fusion elementwise | flops 12800 | bytes 153600 | tf_op jit(solution)/shard_map/add | solution.py:107
  (18 shorter events, 0.1 us)
Async XLA Ops:
  0.0 7.8 %collective-permute-start.1 = (bf16[80,160]{1,0:T(8,128)(2,1)}, bf16[80,160]{1,0:T(8,128)(2,1)S(1)}, u32[]{:S(2)}, u32[]{:S(2)}) collective-permute-start(bf16[80,160]{1,0:T(8,128)(2,1)} %refs_0_.1), channel_id=1, source_target_pairs={{0,3},{1,2},{2,1},{3,0},{4,7},{5,6},{6,5},{7,4},{8,11},{9,10},{10,... | collective-permute-start | bytes 76808 | tf_op jit(solution)/shard_map/ppermute | solution.py:87
  5.1 5.1 %collective-permute-start = (bf16[80,160]{1,0:T(8,128)(2,1)}, bf16[80,160]{1,0:T(8,128)(2,1)S(1)}, u32[]{:S(2)}, u32[]{:S(2)}) collective-permute-start(bf16[80,160]{1,0:T(8,128)(2,1)} %refs_0_.1), channel_id=1, source_target_pairs={{0,2},{1,3},{2,0},{3,1},{4,6},{5,7},{6,4},{7,5},{8,10},{9,11},{10,... | collective-permute-start | bytes 76808 | tf_op jit(solution)/shard_map/ppermute | solution.py:87
  5.1 5.1 %collective-permute-start.2 = (bf16[80,160]{1,0:T(8,128)(2,1)}, bf16[80,160]{1,0:T(8,128)(2,1)S(1)}, u32[]{:S(2)}, u32[]{:S(2)}) collective-permute-start(bf16[80,160]{1,0:T(8,128)(2,1)} %refs_0_.1), channel_id=1, source_target_pairs={{0,1},{1,0},{2,3},{3,2},{4,5},{5,4},{6,7},{7,6},{8,9},{9,8},{10,11... | collective-permute-start | bytes 76808 | tf_op jit(solution)/shard_map/ppermute | solution.py:87
  6.0 0.7 %copy-start.1 = (s32[5,5]{1,0:T(8,128)S(1)}, s32[5,5]{1,0:T(8,128)}, u32[]{:S(2)}) copy-start(s32[5,5]{1,0:T(8,128)} %param.5) | copy-start | bytes 304
  6.7 0.7 %copy-start.2 = (s32[5,5]{1,0:T(8,128)S(1)}, s32[5,5]{1,0:T(8,128)}, u32[]{:S(2)}) copy-start(s32[5,5]{1,0:T(8,128)} %param.6) | copy-start | bytes 304
  7.4 2.8 %copy-start = (bf16[80,160]{1,0:T(8,128)(2,1)S(1)}, bf16[80,160]{1,0:T(8,128)(2,1)}, u32[]{:S(2)}) copy-start(bf16[80,160]{1,0:T(8,128)(2,1)} %refs_0_.1) | copy-start | bytes 76804
  7.8 6.2 %copy-start.3 = (s32[5,5]{1,0:T(8,128)S(1)}, s32[5,5]{1,0:T(8,128)}, u32[]{:S(2)}) copy-start(s32[5,5]{1,0:T(8,128)} %param.7) | copy-start | bytes 304
  10.3 4.0 %collective-permute-start.6 = (bf16[80,640]{1,0:T(8,128)(2,1)S(1)}, bf16[80,640]{1,0:T(8,128)(2,1)S(1)}, u32[]{:S(2)}, u32[]{:S(2)}) collective-permute-start(bf16[80,640]{1,0:T(8,128)(2,1)S(1)} %shard_map.46.refs_0_), channel_id=1, source_target_pairs={{0,4},{4,0},{8,12},{12,8},{16,20},{20,16},{24,28},{28,24},{1,5},{5... | collective-permute-start | bytes 307208 | tf_op jit(solution)/shard_map/ppermute | solution.py:87
  10.4 5.3 %collective-permute-start.5 = (bf16[80,640]{1,0:T(8,128)(2,1)S(1)}, bf16[80,640]{1,0:T(8,128)(2,1)S(1)}, u32[]{:S(2)}, u32[]{:S(2)}) collective-permute-start(bf16[80,640]{1,0:T(8,128)(2,1)S(1)} %shard_map.46.refs_0_), channel_id=1, source_target_pairs={{0,16},{4,20},{8,24},{12,28},{16,0},{20,4},{24,8},{28,12},{1,17},{... | collective-permute-start | bytes 307208 | tf_op jit(solution)/shard_map/ppermute | solution.py:87
  12.0 5.8 %collective-permute-start.4 = (bf16[80,640]{1,0:T(8,128)(2,1)S(1)}, bf16[80,640]{1,0:T(8,128)(2,1)S(1)}, u32[]{:S(2)}, u32[]{:S(2)}) collective-permute-start(bf16[80,640]{1,0:T(8,128)(2,1)S(1)} %shard_map.46.refs_0_), channel_id=1, source_target_pairs={{0,8},{4,12},{8,0},{12,4},{16,24},{20,28},{24,16},{28,20},{1,9},{5... | collective-permute-start | bytes 307208 | tf_op jit(solution)/shard_map/ppermute | solution.py:87
  13.5 5.6 %collective-permute-start.3 = (bf16[80,640]{1,0:T(8,128)(2,1)S(1)}, bf16[80,640]{1,0:T(8,128)(2,1)S(1)}, u32[]{:S(2)}, u32[]{:S(2)}) collective-permute-start(bf16[80,640]{1,0:T(8,128)(2,1)S(1)} %shard_map.46.refs_0_), channel_id=1, source_target_pairs={{0,24},{4,28},{8,16},{12,20},{16,8},{20,12},{24,0},{28,4},{1,25},{... | collective-permute-start | bytes 307208 | tf_op jit(solution)/shard_map/ppermute | solution.py:87
  19.6 1.3 %collective-permute-start.7 = (f32[80,160]{1,0:T(8,128)S(1)}, f32[80,160]{1,0:T(8,128)S(1)}, u32[]{:S(2)}, u32[]{:S(2)}) collective-permute-start(f32[80,160]{1,0:T(8,128)S(1)} %get-tuple-element.8), channel_id=1, source_target_pairs={{0,4},{4,0},{8,12},{12,8},{16,20},{20,16},{24,28},{28,24},{1,5},{5... | collective-permute-start | bytes 153608 | tf_op jit(solution)/shard_map/ppermute | solution.py:87

commit v3 on v2

v3 whole, which is shorter than its diff:
```python
import functools

import jax
import jax.numpy as jnp
from jax import lax
from jax.experimental import pallas as pl
from jax.experimental.pallas import tpu as pltpu
from jax.sharding import PartitionSpec as P


TILE = 128
SMALL = 4 * 1024 * 1024
PARAMS = pltpu.CompilerParams(vmem_limit_bytes=8 * 1024 * 1024)


def lookup(table, rows, cols):
    tiles = jnp.arange(table.shape[0], dtype=jnp.int32)
    row_pick = (rows[:, None] // TILE == tiles[None, :]).astype(jnp.bfloat16)
    col_pick = (tiles[:, None] == cols[None, :] // TILE).astype(jnp.bfloat16)
    left = jnp.dot(row_pick, table.astype(jnp.bfloat16))
    return jnp.dot(left, col_pick)


def span(start, count):
    return jnp.arange(count, dtype=jnp.int32) + start


def gathered(density, occupancy, square_filter, cube_filter):
    b, w = density.shape
    rows = span(lax.axis_index("rows") * b, b)
    cols = span(lax.axis_index("cols") * w, w)
    occupied = density * lookup(occupancy, rows, cols).astype(density.dtype)
    panel = lax.all_gather(occupied, "cols", axis=1, tiled=True)
    column = lax.all_gather(occupied, "rows", axis=0, tiled=True)
    total = jnp.dot(panel, column, preferred_element_type=jnp.float32)
    square = jnp.where(lookup(square_filter, rows, cols) > 0.5, total, 0.0).astype(jnp.bfloat16)
    square_rows = lax.all_gather(square, "cols", axis=1, tiled=True)
    cube = jnp.dot(square_rows, column, preferred_element_type=jnp.float32)
    cube = jnp.where(lookup(cube_filter, rows, cols) > 0.5, cube, 0.0)
    return 3.0 * square.astype(jnp.float32) - 2.0 * cube


def call(kernel, outs, args, scratch=()):
    held = [pltpu.with_memory_space_constraint(x, pltpu.VMEM) for x in args]
    spec = pl.BlockSpec(memory_space=pltpu.VMEM)
    return pl.pallas_call(
        kernel,
        out_shape=outs,
        in_specs=[spec] * len(held),
        out_specs=jax.tree.map(lambda _: spec, outs),
        scratch_shapes=scratch,
        compiler_params=PARAMS,
    )(*held)


def group_turn():
    return (lax.axis_index("rows") // 2) ^ lax.axis_index("cols")


def nt(a, b):
    return lax.dot_general(a, b, (((1,), (1,)), ((), ())), preferred_element_type=jnp.float32)


def without(store, skip):
    n = store.shape[0]
    return jnp.concatenate([store[p + (skip <= p).astype(jnp.int32)] for p in range(n - 1)], axis=1)


def panel_kernel(*refs, shifts, ways):
    n = len(shifts)
    pieces, stored, panel, messages, store = refs[:n], refs[n], refs[n + 1], refs[n + 2 : -1], refs[-1]
    w = pieces[0].shape[1]
    keep = stored[...]
    for p, s in enumerate(shifts):
        store[s] = pieces[p][...] * keep[:, p * w : (p + 1) * w]
    turn = group_turn()
    for f, message in zip(ways, messages):
        message[...] = without(store, turn ^ (f // 2))
    panel[...] = jnp.concatenate([store[s] for s in range(n)], axis=1)


def finish(square, right, pick, cube_keep):
    cube = jnp.dot(square, right, preferred_element_type=jnp.float32)
    own = jnp.dot(square, pick[...], preferred_element_type=jnp.float32)
    return 3.0 * own - 2.0 * jnp.where(cube_keep[...] > 0, cube, 0.0)


def prep_kernel(panel, other, keep, cube_keep, pick, part, left_out, total, known_out, store, *, ways):
    n, _, w = store.shape
    b = panel.shape[0]
    mine, theirs = panel[...], other[...]
    left = jnp.concatenate([mine, theirs], axis=0)
    even = lax.axis_index("rows") % 2 == 1
    turn = group_turn()
    for q in range(n):
        store[q] = left[:, q * w : (q + 1) * w]
    left_out[...] = without(store, turn)
    known = []
    for f in ways:
        block = store[turn ^ (f // 2)]
        half = jnp.where(even, block[:, b:], block[:, :b])
        known.append(jnp.where(even, half, jnp.concatenate([half[b:], half[:b]], axis=0)))
    known = jnp.concatenate(known, axis=1)
    total[...] = jnp.dot(store[turn], known, preferred_element_type=jnp.float32)
    known_out[...] = known.astype(jnp.float32).T.astype(jnp.bfloat16)
    square = jnp.where(keep[...] > 0, nt(left, mine), 0.0).astype(jnp.bfloat16)
    part[...] = finish(square, mine[:, :w], pick, cube_keep)


def part_kernel(part, left, total, known, keep, cube_keep, pick, *refs):
    messages, (mine, yours) = refs[:-2], refs[-2:]
    b, w = mine.shape
    rows = jnp.concatenate([x[...] for x in messages], axis=0)
    square = jnp.where(keep[...] > 0, nt(left[...], rows) + total[...], 0.0).astype(jnp.bfloat16)
    right = jnp.where(group_turn() == 0, known[...], rows[:, :w])
    out = part[...] + finish(square, right, pick, cube_keep)
    mine[...] = out[:b]
    yours[...] = out[b:]


def turns(n):
    return [n - 1] + list(range(1, n - 1)) + [0]


def flips(n_rows):
    return list(range(n_rows - 1, 0, -2))


def permuted(density, occupancy, square_filter, cube_filter):
    b, w = density.shape
    n_rows, n = lax.axis_size("rows"), lax.axis_size("cols")
    j = lax.axis_index("cols")
    me = lax.axis_index("rows") ^ 1

    def swap(x, row_flip, col_flip):
        pairs = [(p * n + q, (p ^ row_flip) * n + (q ^ col_flip)) for p in range(n_rows) for q in range(n)]
        return lax.ppermute(x, ("rows", "cols"), pairs)

    shifts = turns(n)
    pieces = [swap(density, 1, s) for s in shifts]
    order = jnp.concatenate([span((j ^ s) * w, w) for s in shifts])
    rows = span(me * b, b)
    stored = lookup(occupancy, rows, order).astype(jnp.bfloat16)

    far = flips(n_rows)[:-1]
    held = lambda h, k, dtype=jnp.bfloat16: pltpu.VMEM((h, k), dtype)
    outs = [held(b, n * w)] + [held(b, (n - 1) * w)] * len(far)
    kernel = functools.partial(panel_kernel, shifts=shifts, ways=far)
    panel, *messages = call(kernel, outs, [*pieces, stored], [pltpu.VMEM((n, b, w), density.dtype)])
    got = [swap(x, f, 0) for f, x in zip(far, messages)]
    other = swap(panel, 1, 0)

    panel, square_filter, cube_filter = lax.optimization_barrier((panel, square_filter, cube_filter))
    kept = jnp.concatenate([span((me ^ f) * b, b) for f in far])
    pair = jnp.concatenate([rows, span((me ^ 1) * b, b)])
    cols = span(j * w, w)
    cube_keep = lookup(cube_filter, pair, cols)
    pick = lambda x: (x[:, None] == cols[None, :]).astype(jnp.bfloat16)
    height, width = 2 * b, len(far) * b
    outs = [held(height, w, jnp.float32), held(height, (n - 1) * w), held(height, width, jnp.float32), held(width, w)]
    args = [panel, other, lookup(square_filter, pair, rows), cube_keep, pick(rows)]
    store = [pltpu.VMEM((n, height, w), density.dtype)]
    ready = call(functools.partial(prep_kernel, ways=far), outs, args, store)
    args = [*ready, lookup(square_filter, pair, kept), cube_keep, pick(kept), *got]
    ends = [held(b, w, jnp.float32)] * 2
    mine, yours = call(part_kernel, ends, args)
    return yours + swap(mine, 1, 0)


def solution(mesh):
    n_rows, n_cols = mesh.shape["rows"], mesh.shape["cols"]

    def on_device(density, *tables):
        powers = all(k & (k - 1) == 0 for k in (n_rows, n_cols))
        small = density.size * n_rows * n_cols * density.dtype.itemsize <= SMALL
        b, w = density.shape
        fits = small and powers and n_rows == 2 * n_cols and w == 2 * b and b % 16 == 0
        return (permuted if fits else gathered)(density, *tables)

    placed = (P("rows", "cols"), P(), P(), P())
    return jax.shard_map(
        on_device, mesh=mesh, in_specs=placed, out_specs=P("rows", "cols"), check_vma=False
    )
```

time: 21.8 us -> 20.1 us (0.922)
  waiting for transfers between devices: 8.43 us -> 5.68 us
  Pallas kernels: 0.65 us -> 1.41 us
  matrix products: 1.02 us -> 1.32 us
  starting transfers between devices: 9.34 us -> 9.08 us
    ppermute x8 -> x9, waiting for transfers between devices: 8.43 us -> 5.68 us  [swap(): return lax.ppermute(x, ('rows', 'cols'), pairs)]
    pallas_call x2 -> x3, Pallas kernels: 0.65 us -> 1.41 us  [call(): pl.pallas_call(kernel, out_shape=outs, in_specs=[spec] * len(held), out_s...]
    ppermute x8 -> x9, starting transfers between devices: 9.34 us -> 9.08 us  [swap(): return lax.ppermute(x, ('rows', 'cols'), pairs)]
    unnamed x8 -> x6, local copies, waits for them, and re-layouts: 0.95 us -> 1.08 us
    dot_general x3 -> x4, matrix products: 1.02 us -> 1.11 us  [lookup(): return jnp.dot(left, col_pick)]
  transfers between devices with their start and end apart: 8 -> 9, of which waited for: 5 -> 5; matrix products, arithmetic and copies ran while one was open for 7% -> 9% of each run, Pallas kernels for 0% -> 3%
where the time goes in v3:
time: 20.1 us; the launch traced here: 19.9 us
  starting transfers between devices  9.08 us (45%)
  waiting for transfers between devices  5.68 us (28%)
  Pallas kernels  1.41 us (7%)
  matrix products  1.32 us (7%)
  other arithmetic  1.12 us (6%)
  local copies, waits for them, and re-layouts  1.08 us (5%)
    ppermute x9, starting transfers between devices, swap(): return lax.ppermute(x, ('rows', 'cols'), pairs)  9.08 us
    ppermute x9, waiting for transfers between devices, swap(): return lax.ppermute(x, ('rows', 'cols'), pairs)  5.68 us
    pallas_call x3, Pallas kernels, call(): pl.pallas_call(kernel, out_shape=outs, in_specs=[spec] * len(held), out_s...  1.41 us
    dot_general x4, matrix products, lookup(): return jnp.dot(left, col_pick)  1.11 us
    unnamed x6, local copies, waits for them, and re-layouts  1.08 us
    add x1, other arithmetic, permuted(): return yours + swap(mine, 1, 0)  0.65 us
  transfers between devices with their start and end apart: 9, of which 5 were waited for; matrix products, arithmetic and copies ran while one was open for 9% of the time, Pallas kernels for 3%

profile of v3, /device:TPU:0, one launch (start us, length us, event | category | flops | bytes accessed | tf_op | source)
XLA Modules:
  0.0 19.9 jit_solution(15917434586634863744)
XLA Ops:
  0.0 4.5 %collective-permute-start = (bf16[80,160]{1,0:T(8,128)(2,1)}, bf16[80,160]{1,0:T(8,128)(2,1)S(1)}, u32[]{:S(2)}, u32[]{:S(2)}) collective-permute-start(bf16[80,160]{1,0:T(8,128)(2,1)} %param.4), channel_id=1, source_target_pairs={{0,7},{1,6},{2,5},{3,4},{4,3},{5,2},{6,1},{7,0},{8,15},{9,14},{10,... | collective-permute-start | bytes 76808 | tf_op jit(solution)/shard_map/ppermute | solution.py:137
  4.5 0.8 %collective-permute-start.2 = (bf16[80,160]{1,0:T(8,128)(2,1)}, bf16[80,160]{1,0:T(8,128)(2,1)S(1)}, u32[]{:S(2)}, u32[]{:S(2)}) collective-permute-start(bf16[80,160]{1,0:T(8,128)(2,1)} %param.4), channel_id=1, source_target_pairs={{0,6},{1,7},{2,4},{3,5},{4,2},{5,3},{6,0},{7,1},{8,14},{9,15},{10,... | collective-permute-start | bytes 76808 | tf_op jit(solution)/shard_map/ppermute | solution.py:137
  5.6 0.1 compare_convert_fusion.pick
  5.9 0.6 %copy-done = s32[5,5]{1,0:T(8,128)S(1)} copy-done((s32[5,5]{1,0:T(8,128)S(1)}, s32[5,5]{1,0:T(8,128)}, u32[]{:S(2)}) %copy-start) | copy-done | bytes 124
  6.5 0.3 %fusion.3.refs_4_ = bf16[80,640]{1,0:T(8,128)(2,1)S(1)} fusion(s32[80]{0:T(128)S(1)} %and_select_fusion.3, s32[640]{0:T(1024)S(1)} %add_select_fusion, s32[5,5]{1,0:T(8,128)S(1)} %copy-done), kind=kOutput, calls=%fused_computation.2 | convolution fusion | flops 519625 | bytes 105380 | tf_op jit(solution)/shard_map/dot_general | solution.py:21
  6.9 1.3 %collective-permute-done.1.refs_1_ = bf16[80,160]{1,0:T(8,128)(2,1)S(1)} collective-permute-done((bf16[80,160]{1,0:T(8,128)(2,1)}, bf16[80,160]{1,0:T(8,128)(2,1)S(1)}, u32[]{:S(2)}, u32[]{:S(2)}) %collective-permute-start.1) | collective-permute-done | bytes 25632 | tf_op jit(solution)/shard_map/ppermute | solution.py:137
  8.2 1.0 %collective-permute-done.2.refs_2_ = bf16[80,160]{1,0:T(8,128)(2,1)S(1)} collective-permute-done((bf16[80,160]{1,0:T(8,128)(2,1)}, bf16[80,160]{1,0:T(8,128)(2,1)S(1)}, u32[]{:S(2)}, u32[]{:S(2)}) %collective-permute-start.2) | collective-permute-done | bytes 25632 | tf_op jit(solution)/shard_map/ppermute | solution.py:137
  9.2 0.3 %shard_map.46 = (bf16[80,640]{1,0:T(8,128)(2,1)S(1)}, bf16[80,480]{1,0:T(8,128)(2,1)S(1)}, bf16[80,480]{1,0:T(8,128)(2,1)S(1)}, bf16[80,480]{1,0:T(8,128)(2,1)S(1)}) custom-call(bf16[80,160]{1,0:T(8,128)(2,1)S(1)} %collective-permute-done.refs_0_, bf16[80,160]{1,0:T(8,128)(2,1)S(1)} %collective-permute-done.1.refs_1_, ...), custom_call_target="tpu_custom_call" | custom-call | tf_op jit(solution)/shard_map/pallas_call | solution.py:46
  9.5 0.6 %collective-permute-start.4 = (bf16[80,640]{1,0:T(8,128)(2,1)S(1)}, bf16[80,640]{1,0:T(8,128)(2,1)S(1)}, u32[]{:S(2)}, u32[]{:S(2)}) collective-permute-start(bf16[80,640]{1,0:T(8,128)(2,1)S(1)} %get-tuple-element.19.panel), channel_id=1, source_target_pairs={{0,4},{1,5},{2,6},{3,7},{4,0},{5,1},{6,2},{7,3},{8,12},{9,13},{10,... | collective-permute-start | bytes 307208 | tf_op jit(solution)/shard_map/ppermute | solution.py:137
  10.1 2.1 %collective-permute-start.5 = (bf16[80,480]{1,0:T(8,128)(2,1)S(1)}, bf16[80,480]{1,0:T(8,128)(2,1)S(1)}, u32[]{:S(2)}, u32[]{:S(2)}) collective-permute-start(bf16[80,480]{1,0:T(8,128)(2,1)S(1)} %get-tuple-element.26), channel_id=1, source_target_pairs={{0,28},{1,29},{2,30},{3,31},{4,24},{5,25},{6,26},{7,27},{8,20},{9,... | collective-permute-start | bytes 230408 | tf_op jit(solution)/shard_map/ppermute | solution.py:137
  12.2 0.5 %collective-permute-start.6 = (bf16[80,480]{1,0:T(8,128)(2,1)S(1)}, bf16[80,480]{1,0:T(8,128)(2,1)S(1)}, u32[]{:S(2)}, u32[]{:S(2)}) collective-permute-start(bf16[80,480]{1,0:T(8,128)(2,1)S(1)} %get-tuple-element.27), channel_id=1, source_target_pairs={{0,20},{1,21},{2,22},{3,23},{4,16},{5,17},{6,18},{7,19},{8,28},{9,... | collective-permute-start | bytes 230408 | tf_op jit(solution)/shard_map/ppermute | solution.py:137
  12.8 0.2 %collective-permute-start.7 = (bf16[80,480]{1,0:T(8,128)(2,1)S(1)}, bf16[80,480]{1,0:T(8,128)(2,1)S(1)}, u32[]{:S(2)}, u32[]{:S(2)}) collective-permute-start(bf16[80,480]{1,0:T(8,128)(2,1)S(1)} %get-tuple-element.28), channel_id=1, source_target_pairs={{0,12},{1,13},{2,14},{3,15},{4,8},{5,9},{6,10},{7,11},{8,4},{9,5},... | collective-permute-start | bytes 230408 | tf_op jit(solution)/shard_map/ppermute | solution.py:137
  13.0 0.2 %fusion.6 = bf16[160,5]{0,1:T(8,128)(2,1)S(1)} fusion(s32[160]{0:T(256)S(1)} %get-tuple-element.36, s32[5,5]{1,0:T(8,128)S(1)} %copy-done.2), kind=kOutput, calls=%fused_computation.6 | convolution fusion | flops 8825 | bytes 2340 | tf_op jit(solution)/shard_map/dot_general | solution.py:20
  13.2 0.5 %copy-done.1 = s32[5,5]{1,0:T(8,128)S(1)} copy-done((s32[5,5]{1,0:T(8,128)S(1)}, s32[5,5]{1,0:T(8,128)}, u32[]{:S(2)}) %copy-start.1) | copy-done | bytes 124
  13.7 0.3 %fusion.cube_keep = bf16[160,160]{1,0:T(8,128)(2,1)S(1)} fusion(s32[160]{0:T(256)S(1)} %get-tuple-element.36, s32[160]{0:T(256)S(1)} %get-tuple-element.35, s32[5,5]{1,0:T(8,128)S(1)} %copy-done.1), kind=kOutput, calls=%fused_computation | convolution fusion | flops 265625 | bytes 52580 | tf_op jit(solution)/shard_map/dot_general | solution.py:21
  14.0 0.2 %fusion.13.keep = bf16[160,240]{1,0:T(8,128)(2,1)S(1)} fusion(bf16[160,5]{0,1:T(8,128)(2,1)S(1)} %fusion.6, s32[240]{0:T(256)S(1)} %get-tuple-element.31), kind=kOutput, calls=%fused_computation.16 | convolution fusion | flops 385200 | bytes 79360 | tf_op jit(solution)/shard_map/dot_general | solution.py:21
  14.3 0.2 %fusion.18.keep = bf16[160,80]{1,0:T(8,128)(2,1)S(1)} fusion(bf16[160,5]{0,1:T(8,128)(2,1)S(1)} %fusion.6, s32[80]{0:T(128)S(1)} %and_select_fusion.3), kind=kOutput, calls=%fused_computation.28 | convolution fusion | flops 128400 | bytes 27520 | tf_op jit(solution)/shard_map/dot_general | solution.py:21
  14.5 0.7 %shard_map.47 = (f32[160,160]{1,0:T(8,128)S(1)}, bf16[160,480]{1,0:T(8,128)(2,1)S(1)}, f32[160,240]{1,0:T(8,128)S(1)}, bf16[240,160]{1,0:T(8,128)(2,1)S(1)}) custom-call(bf16[80,640]{1,0:T(8,128)(2,1)S(1)} %get-tuple-element.19.panel, bf16[80,640]{1,0:T(8,128)(2,1)S(1)} %collective-permute-done.4.other, bf16[160,80]{1,0:T(8,128)(2,1)S(1)} %fusion.18.keep, ...), custom_call_target="tpu_custom_call" | custom-call | tf_op jit(solution)/shard_map/pallas_call | solution.py:46
  15.2 0.3 %collective-permute-done.5.refs_0_ = bf16[80,480]{1,0:T(8,128)(2,1)S(1)} collective-permute-done((bf16[80,480]{1,0:T(8,128)(2,1)S(1)}, bf16[80,480]{1,0:T(8,128)(2,1)S(1)}, u32[]{:S(2)}, u32[]{:S(2)}) %collective-permute-start.5) | collective-permute-done | bytes 76832 | tf_op jit(solution)/shard_map/ppermute | solution.py:137
  15.5 1.9 %collective-permute-done.6.refs_1_ = bf16[80,480]{1,0:T(8,128)(2,1)S(1)} collective-permute-done((bf16[80,480]{1,0:T(8,128)(2,1)S(1)}, bf16[80,480]{1,0:T(8,128)(2,1)S(1)}, u32[]{:S(2)}, u32[]{:S(2)}) %collective-permute-start.6) | collective-permute-done | bytes 76832 | tf_op jit(solution)/shard_map/ppermute | solution.py:137
  17.4 0.5 %shard_map.48 = (f32[80,160]{1,0:T(8,128)S(1)}, f32[80,160]{1,0:T(8,128)S(1)}) custom-call(f32[160,160]{1,0:T(8,128)S(1)} %get-tuple-element.22.part, bf16[160,480]{1,0:T(8,128)(2,1)S(1)} %get-tuple-element.23.left, f32[160,240]{1,0:T(8,128)S(1)} %get-tuple-element.24.total, bf16[240,160]{1,0:T(8,128)(2,1)S(1)} %get-tuple-element.25.known, ...), custom_call_target="tpu_custom_call" | custom-call | tf_op jit(solution)/shard_map/pallas_call | solution.py:46
  17.9 0.2 collective-permute-start.8
  18.1 1.2 %collective-permute-done.8 = f32[80,160]{1,0:T(8,128)S(1)} collective-permute-done((f32[80,160]{1,0:T(8,128)S(1)}, f32[80,160]{1,0:T(8,128)S(1)}, u32[]{:S(2)}, u32[]{:S(2)}) %collective-permute-start.8) | collective-permute-done | bytes 51232 | tf_op jit(solution)/shard_map/ppermute | solution.py:137
  19.2 0.6 %add.176 = f32[80,160]{1,0:T(8,128)} add(f32[80,160]{1,0:T(8,128)S(1)} %get-tuple-element.29, f32[80,160]{1,0:T(8,128)S(1)} %collective-permute-done.8) | non-fusion elementwise | flops 12800 | bytes 153600 | tf_op jit(solution)/shard_map/add | solution.py:167
  (22 shorter events, 0.4 us)
Async XLA Ops:
  0.0 6.9 %collective-permute-start = (bf16[80,160]{1,0:T(8,128)(2,1)}, bf16[80,160]{1,0:T(8,128)(2,1)S(1)}, u32[]{:S(2)}, u32[]{:S(2)}) collective-permute-start(bf16[80,160]{1,0:T(8,128)(2,1)} %param.4), channel_id=1, source_target_pairs={{0,7},{1,6},{2,5},{3,4},{4,3},{5,2},{6,1},{7,0},{8,15},{9,14},{10,... | collective-permute-start | bytes 76808 | tf_op jit(solution)/shard_map/ppermute | solution.py:137
  4.5 3.6 %collective-permute-start.1 = (bf16[80,160]{1,0:T(8,128)(2,1)}, bf16[80,160]{1,0:T(8,128)(2,1)S(1)}, u32[]{:S(2)}, u32[]{:S(2)}) collective-permute-start(bf16[80,160]{1,0:T(8,128)(2,1)} %param.4), channel_id=1, source_target_pairs={{0,5},{1,4},{2,7},{3,6},{4,1},{5,0},{6,3},{7,2},{8,13},{9,12},{10,... | collective-permute-start | bytes 76808 | tf_op jit(solution)/shard_map/ppermute | solution.py:137
  4.5 4.6 %collective-permute-start.2 = (bf16[80,160]{1,0:T(8,128)(2,1)}, bf16[80,160]{1,0:T(8,128)(2,1)S(1)}, u32[]{:S(2)}, u32[]{:S(2)}) collective-permute-start(bf16[80,160]{1,0:T(8,128)(2,1)} %param.4), channel_id=1, source_target_pairs={{0,6},{1,7},{2,4},{3,5},{4,2},{5,3},{6,0},{7,1},{8,14},{9,15},{10,... | collective-permute-start | bytes 76808 | tf_op jit(solution)/shard_map/ppermute | solution.py:137
  5.4 3.8 %collective-permute-start.3 = (bf16[80,160]{1,0:T(8,128)(2,1)}, bf16[80,160]{1,0:T(8,128)(2,1)S(1)}, u32[]{:S(2)}, u32[]{:S(2)}) collective-permute-start(bf16[80,160]{1,0:T(8,128)(2,1)} %param.4), channel_id=1, source_target_pairs={{0,4},{1,5},{2,6},{3,7},{4,0},{5,1},{6,2},{7,3},{8,12},{9,13},{10,... | collective-permute-start | bytes 76808 | tf_op jit(solution)/shard_map/ppermute | solution.py:137
  5.8 0.7 %copy-start = (s32[5,5]{1,0:T(8,128)S(1)}, s32[5,5]{1,0:T(8,128)}, u32[]{:S(2)}) copy-start(s32[5,5]{1,0:T(8,128)} %param.5) | copy-start | bytes 304
  9.5 3.5 %copy-start.2 = (s32[5,5]{1,0:T(8,128)S(1)}, s32[5,5]{1,0:T(8,128)}, u32[]{:S(2)}) copy-start(s32[5,5]{1,0:T(8,128)} %param.6) | copy-start | bytes 304
  9.5 5.0 %collective-permute-start.4 = (bf16[80,640]{1,0:T(8,128)(2,1)S(1)}, bf16[80,640]{1,0:T(8,128)(2,1)S(1)}, u32[]{:S(2)}, u32[]{:S(2)}) collective-permute-start(bf16[80,640]{1,0:T(8,128)(2,1)S(1)} %get-tuple-element.19.panel), channel_id=1, source_target_pairs={{0,4},{1,5},{2,6},{3,7},{4,0},{5,1},{6,2},{7,3},{8,12},{9,13},{10,... | collective-permute-start | bytes 307208 | tf_op jit(solution)/shard_map/ppermute | solution.py:137
  10.1 5.4 %collective-permute-start.5 = (bf16[80,480]{1,0:T(8,128)(2,1)S(1)}, bf16[80,480]{1,0:T(8,128)(2,1)S(1)}, u32[]{:S(2)}, u32[]{:S(2)}) collective-permute-start(bf16[80,480]{1,0:T(8,128)(2,1)S(1)} %get-tuple-element.26), channel_id=1, source_target_pairs={{0,28},{1,29},{2,30},{3,31},{4,24},{5,25},{6,26},{7,27},{8,20},{9,... | collective-permute-start | bytes 230408 | tf_op jit(solution)/shard_map/ppermute | solution.py:137
  12.2 5.2 %collective-permute-start.6 = (bf16[80,480]{1,0:T(8,128)(2,1)S(1)}, bf16[80,480]{1,0:T(8,128)(2,1)S(1)}, u32[]{:S(2)}, u32[]{:S(2)}) collective-permute-start(bf16[80,480]{1,0:T(8,128)(2,1)S(1)} %get-tuple-element.27), channel_id=1, source_target_pairs={{0,20},{1,21},{2,22},{3,23},{4,16},{5,17},{6,18},{7,19},{8,28},{9,... | collective-permute-start | bytes 230408 | tf_op jit(solution)/shard_map/ppermute | solution.py:137
  12.8 4.6 %collective-permute-start.7 = (bf16[80,480]{1,0:T(8,128)(2,1)S(1)}, bf16[80,480]{1,0:T(8,128)(2,1)S(1)}, u32[]{:S(2)}, u32[]{:S(2)}) collective-permute-start(bf16[80,480]{1,0:T(8,128)(2,1)S(1)} %get-tuple-element.28), channel_id=1, source_target_pairs={{0,12},{1,13},{2,14},{3,15},{4,8},{5,9},{6,10},{7,11},{8,4},{9,5},... | collective-permute-start | bytes 230408 | tf_op jit(solution)/shard_map/ppermute | solution.py:137
  13.0 0.7 %copy-start.1 = (s32[5,5]{1,0:T(8,128)S(1)}, s32[5,5]{1,0:T(8,128)}, u32[]{:S(2)}) copy-start(s32[5,5]{1,0:T(8,128)} %param.7) | copy-start | bytes 304
  17.9 1.3 %collective-permute-start.8 = (f32[80,160]{1,0:T(8,128)S(1)}, f32[80,160]{1,0:T(8,128)S(1)}, u32[]{:S(2)}, u32[]{:S(2)}) collective-permute-start(f32[80,160]{1,0:T(8,128)S(1)} %get-tuple-element.30), channel_id=1, source_target_pairs={{0,4},{1,5},{2,6},{3,7},{4,0},{5,1},{6,2},{7,3},{8,12},{9,13},{10,... | collective-permute-start | bytes 153608 | tf_op jit(solution)/shard_map/ppermute | solution.py:137

commit v4 on v3

--- a/solution.py
+++ b/solution.py
@@ -68,15 +68,15 @@
 
 def panel_kernel(*refs, shifts, ways):
     n = len(shifts)
-    pieces, stored, panel, messages, store = refs[:n], refs[n], refs[n + 1], refs[n + 2 : -1], refs[-1]
+    pieces, stored, panel, messages = dict(zip(shifts, refs)), refs[n], refs[n + 1], refs[n + 2 :]
     w = pieces[0].shape[1]
-    keep = stored[...]
-    for p, s in enumerate(shifts):
-        store[s] = pieces[p][...] * keep[:, p * w : (p + 1) * w]
+    whole = jnp.concatenate([pieces[s][...] for s in range(n)], axis=1) * stored[...]
+    panel[...] = whole
+    ahead, behind = whole[:, : (n - 1) * w], whole[:, w:]
+    lane = lax.broadcasted_iota(jnp.int32, ahead.shape, 1)
     turn = group_turn()
     for f, message in zip(ways, messages):
-        message[...] = without(store, turn ^ (f // 2))
-    panel[...] = jnp.concatenate([store[s] for s in range(n)], axis=1)
+        message[...] = jnp.where(lane < (turn ^ (f // 2)) * w, ahead, behind)
 
 
 def finish(square, right, pick, cube_keep):
@@ -138,7 +138,7 @@
 
     shifts = turns(n)
     pieces = [swap(density, 1, s) for s in shifts]
-    order = jnp.concatenate([span((j ^ s) * w, w) for s in shifts])
+    order = jnp.concatenate([span((j ^ s) * w, w) for s in range(n)])
     rows = span(me * b, b)
     stored = lookup(occupancy, rows, order).astype(jnp.bfloat16)
 
@@ -146,7 +146,7 @@
     held = lambda h, k, dtype=jnp.bfloat16: pltpu.VMEM((h, k), dtype)
     outs = [held(b, n * w)] + [held(b, (n - 1) * w)] * len(far)
     kernel = functools.partial(panel_kernel, shifts=shifts, ways=far)
-    panel, *messages = call(kernel, outs, [*pieces, stored], [pltpu.VMEM((n, b, w), density.dtype)])
+    panel, *messages = call(kernel, outs, [*pieces, stored])
     got = [swap(x, f, 0) for f, x in zip(far, messages)]
     other = swap(panel, 1, 0)
 

time: 20.1 us -> 20 us (level)
  no operation moved by 1% of the time
where the time goes in v4:
time: 20 us; the launch traced here: 19.8 us
  starting transfers between devices  9.08 us (45%)
  waiting for transfers between devices  5.68 us (28%)
  matrix products  1.31 us (7%)
  Pallas kernels  1.31 us (7%)
  other arithmetic  1.12 us (6%)
  local copies, waits for them, and re-layouts  1.08 us (5%)
    ppermute x9, starting transfers between devices, swap(): return lax.ppermute(x, ('rows', 'cols'), pairs)  9.08 us
    ppermute x9, waiting for transfers between devices, swap(): return lax.ppermute(x, ('rows', 'cols'), pairs)  5.68 us
    pallas_call x3, Pallas kernels, call(): pl.pallas_call(kernel, out_shape=outs, in_specs=[spec] * len(held), out_s...  1.31 us
    dot_general x4, matrix products, lookup(): return jnp.dot(left, col_pick)  1.11 us
    unnamed x6, local copies, waits for them, and re-layouts  1.08 us
    add x1, other arithmetic, permuted(): return yours + swap(mine, 1, 0)  0.65 us
  transfers between devices with their start and end apart: 9, of which 5 were waited for; matrix products, arithmetic and copies ran while one was open for 9% of the time, Pallas kernels for 3%

profile of v4, /device:TPU:0, one launch (start us, length us, event | category | flops | bytes accessed | tf_op | source)
XLA Modules:
  0.0 19.8 jit_solution(14029437441098107266)
XLA Ops:
  0.0 4.5 %collective-permute-start = (bf16[80,160]{1,0:T(8,128)(2,1)}, bf16[80,160]{1,0:T(8,128)(2,1)S(1)}, u32[]{:S(2)}, u32[]{:S(2)}) collective-permute-start(bf16[80,160]{1,0:T(8,128)(2,1)} %param.4), channel_id=1, source_target_pairs={{0,7},{1,6},{2,5},{3,4},{4,3},{5,2},{6,1},{7,0},{8,15},{9,14},{10,... | collective-permute-start | bytes 76808 | tf_op jit(solution)/shard_map/ppermute | solution.py:137
  4.5 0.8 %collective-permute-start.2 = (bf16[80,160]{1,0:T(8,128)(2,1)}, bf16[80,160]{1,0:T(8,128)(2,1)S(1)}, u32[]{:S(2)}, u32[]{:S(2)}) collective-permute-start(bf16[80,160]{1,0:T(8,128)(2,1)} %param.4), channel_id=1, source_target_pairs={{0,6},{1,7},{2,4},{3,5},{4,2},{5,3},{6,0},{7,1},{8,14},{9,15},{10,... | collective-permute-start | bytes 76808 | tf_op jit(solution)/shard_map/ppermute | solution.py:137
  5.6 0.1 compare_convert_fusion.pick
  5.9 0.6 %copy-done = s32[5,5]{1,0:T(8,128)S(1)} copy-done((s32[5,5]{1,0:T(8,128)S(1)}, s32[5,5]{1,0:T(8,128)}, u32[]{:S(2)}) %copy-start) | copy-done | bytes 124
  6.5 0.3 %fusion.3.refs_4_ = bf16[80,640]{1,0:T(8,128)(2,1)S(1)} fusion(s32[80]{0:T(128)S(1)} %and_select_fusion.3, s32[640]{0:T(1024)S(1)} %add_select_fusion, s32[5,5]{1,0:T(8,128)S(1)} %copy-done), kind=kOutput, calls=%fused_computation.2 | convolution fusion | flops 519625 | bytes 105380 | tf_op jit(solution)/shard_map/dot_general | solution.py:21
  6.9 1.3 %collective-permute-done.1.refs_1_ = bf16[80,160]{1,0:T(8,128)(2,1)S(1)} collective-permute-done((bf16[80,160]{1,0:T(8,128)(2,1)}, bf16[80,160]{1,0:T(8,128)(2,1)S(1)}, u32[]{:S(2)}, u32[]{:S(2)}) %collective-permute-start.1) | collective-permute-done | bytes 25632 | tf_op jit(solution)/shard_map/ppermute | solution.py:137
  8.2 1.0 %collective-permute-done.2.refs_2_ = bf16[80,160]{1,0:T(8,128)(2,1)S(1)} collective-permute-done((bf16[80,160]{1,0:T(8,128)(2,1)}, bf16[80,160]{1,0:T(8,128)(2,1)S(1)}, u32[]{:S(2)}, u32[]{:S(2)}) %collective-permute-start.2) | collective-permute-done | bytes 25632 | tf_op jit(solution)/shard_map/ppermute | solution.py:137
  9.2 0.2 shard_map.46
  9.4 0.6 %collective-permute-start.4 = (bf16[80,640]{1,0:T(8,128)(2,1)S(1)}, bf16[80,640]{1,0:T(8,128)(2,1)S(1)}, u32[]{:S(2)}, u32[]{:S(2)}) collective-permute-start(bf16[80,640]{1,0:T(8,128)(2,1)S(1)} %get-tuple-element.19.panel), channel_id=1, source_target_pairs={{0,4},{1,5},{2,6},{3,7},{4,0},{5,1},{6,2},{7,3},{8,12},{9,13},{10,... | collective-permute-start | bytes 307208 | tf_op jit(solution)/shard_map/ppermute | solution.py:137
  10.0 2.1 %collective-permute-start.5 = (bf16[80,480]{1,0:T(8,128)(2,1)S(1)}, bf16[80,480]{1,0:T(8,128)(2,1)S(1)}, u32[]{:S(2)}, u32[]{:S(2)}) collective-permute-start(bf16[80,480]{1,0:T(8,128)(2,1)S(1)} %get-tuple-element.26), channel_id=1, source_target_pairs={{0,28},{1,29},{2,30},{3,31},{4,24},{5,25},{6,26},{7,27},{8,20},{9,... | collective-permute-start | bytes 230408 | tf_op jit(solution)/shard_map/ppermute | solution.py:137
  12.1 0.5 %collective-permute-start.6 = (bf16[80,480]{1,0:T(8,128)(2,1)S(1)}, bf16[80,480]{1,0:T(8,128)(2,1)S(1)}, u32[]{:S(2)}, u32[]{:S(2)}) collective-permute-start(bf16[80,480]{1,0:T(8,128)(2,1)S(1)} %get-tuple-element.27), channel_id=1, source_target_pairs={{0,20},{1,21},{2,22},{3,23},{4,16},{5,17},{6,18},{7,19},{8,28},{9,... | collective-permute-start | bytes 230408 | tf_op jit(solution)/shard_map/ppermute | solution.py:137
  12.7 0.2 %collective-permute-start.7 = (bf16[80,480]{1,0:T(8,128)(2,1)S(1)}, bf16[80,480]{1,0:T(8,128)(2,1)S(1)}, u32[]{:S(2)}, u32[]{:S(2)}) collective-permute-start(bf16[80,480]{1,0:T(8,128)(2,1)S(1)} %get-tuple-element.28), channel_id=1, source_target_pairs={{0,12},{1,13},{2,14},{3,15},{4,8},{5,9},{6,10},{7,11},{8,4},{9,5},... | collective-permute-start | bytes 230408 | tf_op jit(solution)/shard_map/ppermute | solution.py:137
  12.9 0.2 %fusion.6 = bf16[160,5]{0,1:T(8,128)(2,1)S(1)} fusion(s32[160]{0:T(256)S(1)} %get-tuple-element.36, s32[5,5]{1,0:T(8,128)S(1)} %copy-done.2), kind=kOutput, calls=%fused_computation.6 | convolution fusion | flops 8825 | bytes 2340 | tf_op jit(solution)/shard_map/dot_general | solution.py:20
  13.1 0.5 %copy-done.1 = s32[5,5]{1,0:T(8,128)S(1)} copy-done((s32[5,5]{1,0:T(8,128)S(1)}, s32[5,5]{1,0:T(8,128)}, u32[]{:S(2)}) %copy-start.1) | copy-done | bytes 124
  13.6 0.3 %fusion.cube_keep = bf16[160,160]{1,0:T(8,128)(2,1)S(1)} fusion(s32[160]{0:T(256)S(1)} %get-tuple-element.36, s32[160]{0:T(256)S(1)} %get-tuple-element.35, s32[5,5]{1,0:T(8,128)S(1)} %copy-done.1), kind=kOutput, calls=%fused_computation | convolution fusion | flops 265625 | bytes 52580 | tf_op jit(solution)/shard_map/dot_general | solution.py:21
  13.9 0.2 %fusion.13.keep = bf16[160,240]{1,0:T(8,128)(2,1)S(1)} fusion(bf16[160,5]{0,1:T(8,128)(2,1)S(1)} %fusion.6, s32[240]{0:T(256)S(1)} %get-tuple-element.31), kind=kOutput, calls=%fused_computation.16 | convolution fusion | flops 385200 | bytes 79360 | tf_op jit(solution)/shard_map/dot_general | solution.py:21
  14.2 0.2 %fusion.18.keep = bf16[160,80]{1,0:T(8,128)(2,1)S(1)} fusion(bf16[160,5]{0,1:T(8,128)(2,1)S(1)} %fusion.6, s32[80]{0:T(128)S(1)} %and_select_fusion.3), kind=kOutput, calls=%fused_computation.28 | convolution fusion | flops 128400 | bytes 27520 | tf_op jit(solution)/shard_map/dot_general | solution.py:21
  14.4 0.7 %shard_map.47 = (f32[160,160]{1,0:T(8,128)S(1)}, bf16[160,480]{1,0:T(8,128)(2,1)S(1)}, f32[160,240]{1,0:T(8,128)S(1)}, bf16[240,160]{1,0:T(8,128)(2,1)S(1)}) custom-call(bf16[80,640]{1,0:T(8,128)(2,1)S(1)} %get-tuple-element.19.panel, bf16[80,640]{1,0:T(8,128)(2,1)S(1)} %collective-permute-done.4.other, bf16[160,80]{1,0:T(8,128)(2,1)S(1)} %fusion.18.keep, ...), custom_call_target="tpu_custom_call" | custom-call | tf_op jit(solution)/shard_map/pallas_call | solution.py:46
  15.1 0.3 %collective-permute-done.5.refs_0_ = bf16[80,480]{1,0:T(8,128)(2,1)S(1)} collective-permute-done((bf16[80,480]{1,0:T(8,128)(2,1)S(1)}, bf16[80,480]{1,0:T(8,128)(2,1)S(1)}, u32[]{:S(2)}, u32[]{:S(2)}) %collective-permute-start.5) | collective-permute-done | bytes 76832 | tf_op jit(solution)/shard_map/ppermute | solution.py:137
  15.4 1.9 %collective-permute-done.6.refs_1_ = bf16[80,480]{1,0:T(8,128)(2,1)S(1)} collective-permute-done((bf16[80,480]{1,0:T(8,128)(2,1)S(1)}, bf16[80,480]{1,0:T(8,128)(2,1)S(1)}, u32[]{:S(2)}, u32[]{:S(2)}) %collective-permute-start.6) | collective-permute-done | bytes 76832 | tf_op jit(solution)/shard_map/ppermute | solution.py:137
  17.3 0.5 %shard_map.48 = (f32[80,160]{1,0:T(8,128)S(1)}, f32[80,160]{1,0:T(8,128)S(1)}) custom-call(f32[160,160]{1,0:T(8,128)S(1)} %get-tuple-element.22.part, bf16[160,480]{1,0:T(8,128)(2,1)S(1)} %get-tuple-element.23.left, f32[160,240]{1,0:T(8,128)S(1)} %get-tuple-element.24.total, bf16[240,160]{1,0:T(8,128)(2,1)S(1)} %get-tuple-element.25.known, ...), custom_call_target="tpu_custom_call" | custom-call | tf_op jit(solution)/shard_map/pallas_call | solution.py:46
  17.8 0.2 collective-permute-start.8
  18.0 1.2 %collective-permute-done.8 = f32[80,160]{1,0:T(8,128)S(1)} collective-permute-done((f32[80,160]{1,0:T(8,128)S(1)}, f32[80,160]{1,0:T(8,128)S(1)}, u32[]{:S(2)}, u32[]{:S(2)}) %collective-permute-start.8) | collective-permute-done | bytes 51232 | tf_op jit(solution)/shard_map/ppermute | solution.py:137
  19.1 0.6 %add.176 = f32[80,160]{1,0:T(8,128)} add(f32[80,160]{1,0:T(8,128)S(1)} %get-tuple-element.29, f32[80,160]{1,0:T(8,128)S(1)} %collective-permute-done.8) | non-fusion elementwise | flops 12800 | bytes 153600 | tf_op jit(solution)/shard_map/add | solution.py:167
  (22 shorter events, 0.4 us)
Async XLA Ops:
  0.0 6.9 %collective-permute-start = (bf16[80,160]{1,0:T(8,128)(2,1)}, bf16[80,160]{1,0:T(8,128)(2,1)S(1)}, u32[]{:S(2)}, u32[]{:S(2)}) collective-permute-start(bf16[80,160]{1,0:T(8,128)(2,1)} %param.4), channel_id=1, source_target_pairs={{0,7},{1,6},{2,5},{3,4},{4,3},{5,2},{6,1},{7,0},{8,15},{9,14},{10,... | collective-permute-start | bytes 76808 | tf_op jit(solution)/shard_map/ppermute | solution.py:137
  4.5 3.6 %collective-permute-start.1 = (bf16[80,160]{1,0:T(8,128)(2,1)}, bf16[80,160]{1,0:T(8,128)(2,1)S(1)}, u32[]{:S(2)}, u32[]{:S(2)}) collective-permute-start(bf16[80,160]{1,0:T(8,128)(2,1)} %param.4), channel_id=1, source_target_pairs={{0,5},{1,4},{2,7},{3,6},{4,1},{5,0},{6,3},{7,2},{8,13},{9,12},{10,... | collective-permute-start | bytes 76808 | tf_op jit(solution)/shard_map/ppermute | solution.py:137
  4.5 4.6 %collective-permute-start.2 = (bf16[80,160]{1,0:T(8,128)(2,1)}, bf16[80,160]{1,0:T(8,128)(2,1)S(1)}, u32[]{:S(2)}, u32[]{:S(2)}) collective-permute-start(bf16[80,160]{1,0:T(8,128)(2,1)} %param.4), channel_id=1, source_target_pairs={{0,6},{1,7},{2,4},{3,5},{4,2},{5,3},{6,0},{7,1},{8,14},{9,15},{10,... | collective-permute-start | bytes 76808 | tf_op jit(solution)/shard_map/ppermute | solution.py:137
  5.4 3.8 %collective-permute-start.3 = (bf16[80,160]{1,0:T(8,128)(2,1)}, bf16[80,160]{1,0:T(8,128)(2,1)S(1)}, u32[]{:S(2)}, u32[]{:S(2)}) collective-permute-start(bf16[80,160]{1,0:T(8,128)(2,1)} %param.4), channel_id=1, source_target_pairs={{0,4},{1,5},{2,6},{3,7},{4,0},{5,1},{6,2},{7,3},{8,12},{9,13},{10,... | collective-permute-start | bytes 76808 | tf_op jit(solution)/shard_map/ppermute | solution.py:137
  5.8 0.7 %copy-start = (s32[5,5]{1,0:T(8,128)S(1)}, s32[5,5]{1,0:T(8,128)}, u32[]{:S(2)}) copy-start(s32[5,5]{1,0:T(8,128)} %param.5) | copy-start | bytes 304
  9.4 3.5 %copy-start.2 = (s32[5,5]{1,0:T(8,128)S(1)}, s32[5,5]{1,0:T(8,128)}, u32[]{:S(2)}) copy-start(s32[5,5]{1,0:T(8,128)} %param.6) | copy-start | bytes 304
  9.4 5.0 %collective-permute-start.4 = (bf16[80,640]{1,0:T(8,128)(2,1)S(1)}, bf16[80,640]{1,0:T(8,128)(2,1)S(1)}, u32[]{:S(2)}, u32[]{:S(2)}) collective-permute-start(bf16[80,640]{1,0:T(8,128)(2,1)S(1)} %get-tuple-element.19.panel), channel_id=1, source_target_pairs={{0,4},{1,5},{2,6},{3,7},{4,0},{5,1},{6,2},{7,3},{8,12},{9,13},{10,... | collective-permute-start | bytes 307208 | tf_op jit(solution)/shard_map/ppermute | solution.py:137
  10.0 5.4 %collective-permute-start.5 = (bf16[80,480]{1,0:T(8,128)(2,1)S(1)}, bf16[80,480]{1,0:T(8,128)(2,1)S(1)}, u32[]{:S(2)}, u32[]{:S(2)}) collective-permute-start(bf16[80,480]{1,0:T(8,128)(2,1)S(1)} %get-tuple-element.26), channel_id=1, source_target_pairs={{0,28},{1,29},{2,30},{3,31},{4,24},{5,25},{6,26},{7,27},{8,20},{9,... | collective-permute-start | bytes 230408 | tf_op jit(solution)/shard_map/ppermute | solution.py:137
  12.1 5.2 %collective-permute-start.6 = (bf16[80,480]{1,0:T(8,128)(2,1)S(1)}, bf16[80,480]{1,0:T(8,128)(2,1)S(1)}, u32[]{:S(2)}, u32[]{:S(2)}) collective-permute-start(bf16[80,480]{1,0:T(8,128)(2,1)S(1)} %get-tuple-element.27), channel_id=1, source_target_pairs={{0,20},{1,21},{2,22},{3,23},{4,16},{5,17},{6,18},{7,19},{8,28},{9,... | collective-permute-start | bytes 230408 | tf_op jit(solution)/shard_map/ppermute | solution.py:137
  12.7 4.6 %collective-permute-start.7 = (bf16[80,480]{1,0:T(8,128)(2,1)S(1)}, bf16[80,480]{1,0:T(8,128)(2,1)S(1)}, u32[]{:S(2)}, u32[]{:S(2)}) collective-permute-start(bf16[80,480]{1,0:T(8,128)(2,1)S(1)} %get-tuple-element.28), channel_id=1, source_target_pairs={{0,12},{1,13},{2,14},{3,15},{4,8},{5,9},{6,10},{7,11},{8,4},{9,5},... | collective-permute-start | bytes 230408 | tf_op jit(solution)/shard_map/ppermute | solution.py:137
  12.9 0.7 %copy-start.1 = (s32[5,5]{1,0:T(8,128)S(1)}, s32[5,5]{1,0:T(8,128)}, u32[]{:S(2)}) copy-start(s32[5,5]{1,0:T(8,128)} %param.7) | copy-start | bytes 304
  17.8 1.3 %collective-permute-start.8 = (f32[80,160]{1,0:T(8,128)S(1)}, f32[80,160]{1,0:T(8,128)S(1)}, u32[]{:S(2)}, u32[]{:S(2)}) collective-permute-start(f32[80,160]{1,0:T(8,128)S(1)} %get-tuple-element.30), channel_id=1, source_target_pairs={{0,4},{1,5},{2,6},{3,7},{4,0},{5,1},{6,2},{7,3},{8,12},{9,13},{10,... | collective-permute-start | bytes 153608 | tf_op jit(solution)/shard_map/ppermute | solution.py:137

commit v5 on v4

--- a/solution.py
+++ b/solution.py
@@ -111,7 +111,12 @@
     messages, (mine, yours) = refs[:-2], refs[-2:]
     b, w = mine.shape
     rows = jnp.concatenate([x[...] for x in messages], axis=0)
-    square = jnp.where(keep[...] > 0, nt(left[...], rows) + total[...], 0.0).astype(jnp.bfloat16)
+    squares = []
+    for k in range(2):
+        at = slice(k * b, (k + 1) * b)
+        product = nt(left[at, :], rows) + total[at, :]
+        squares.append(jnp.where(keep[at, :] > 0, product, 0.0).astype(jnp.bfloat16))
+    square = jnp.concatenate(squares, axis=0)
     right = jnp.where(group_turn() == 0, known[...], rows[:, :w])
     out = part[...] + finish(square, right, pick, cube_keep)
     mine[...] = out[:b]
@@ -124,6 +129,31 @@
 
 def flips(n_rows):
     return list(range(n_rows - 1, 0, -2))
+
+
+def add_kernel(a, b, out, store, done):
+    h = out.shape[0] // 2
+    copies = [pltpu.make_async_copy(store.at[pl.ds(k * h, h)], out.at[pl.ds(k * h, h)], done.at[k]) for k in range(2)]
+    for k, copy in enumerate(copies):
+        at = pl.ds(k * h, h)
+        store[at, :] = a[at, :] + b[at, :]
+        copy.start()
+    for copy in copies:
+        copy.wait()
+
+
+def add(a, b):
+    held = [pltpu.with_memory_space_constraint(x, pltpu.VMEM) for x in (a, b)]
+    spec = pl.BlockSpec(memory_space=pltpu.VMEM)
+    return pl.pallas_call(
+        add_kernel,
+        out_shape=jax.ShapeDtypeStruct(a.shape, a.dtype),
+        in_specs=[spec] * 2,
+        out_specs=pl.BlockSpec(memory_space=pl.ANY),
+        scratch_shapes=[pltpu.VMEM(a.shape, a.dtype), pltpu.SemaphoreType.DMA((2,))],
+        compiler_params=PARAMS,
+        name="add",
+    )(*held)
 
 
 def permuted(density, occupancy, square_filter, cube_filter):
@@ -164,7 +194,7 @@
     args = [*ready, lookup(square_filter, pair, kept), cube_keep, pick(kept), *got]
     ends = [held(b, w, jnp.float32)] * 2
     mine, yours = call(part_kernel, ends, args)
-    return yours + swap(mine, 1, 0)
+    return add(yours, swap(mine, 1, 0))
 
 
 def solution(mesh):

time: 20 us -> 20 us (level)
  other arithmetic: 1.12 us -> 0.47 us
  Pallas kernels: 1.31 us -> 1.95 us
    pallas_call x0 -> x1, Pallas kernels: none -> 0.65 us  [add(): pl.pallas_call(add_kernel, out_shape=jax.ShapeDtypeStruct(a.shape, a.dtyp...]
    add x1 -> x0, other arithmetic: 0.65 us -> none  [permuted(): return yours + swap(mine, 1, 0)]
where the time goes in v5:
time: 20 us; the launch traced here: 19.8 us
  starting transfers between devices  9.08 us (45%)
  waiting for transfers between devices  5.68 us (28%)
  Pallas kernels  1.95 us (10%)
  matrix products  1.31 us (7%)
  local copies, waits for them, and re-layouts  1.08 us (5%)
  other arithmetic  0.47 us (2%)
    ppermute x9, starting transfers between devices, swap(): return lax.ppermute(x, ('rows', 'cols'), pairs)  9.08 us
    ppermute x9, waiting for transfers between devices, swap(): return lax.ppermute(x, ('rows', 'cols'), pairs)  5.68 us
    pallas_call x3, Pallas kernels, call(): pl.pallas_call(kernel, out_shape=outs, in_specs=[spec] * len(held), out_s...  1.29 us
    dot_general x4, matrix products, lookup(): return jnp.dot(left, col_pick)  1.11 us
    unnamed x6, local copies, waits for them, and re-layouts  1.08 us
    pallas_call x1, Pallas kernels, add(): pl.pallas_call(add_kernel, out_shape=jax.ShapeDtypeStruct(a.shape, a.dtyp...  0.65 us
  transfers between devices with their start and end apart: 9, of which 5 were waited for; matrix products, arithmetic and copies ran while one was open for 9% of the time, Pallas kernels for 3%

profile of v5, /device:TPU:0, one launch (start us, length us, event | category | flops | bytes accessed | tf_op | source)
XLA Modules:
  0.0 19.8 jit_solution(9085146384817358838)
XLA Ops:
  0.0 4.5 %collective-permute-start = (bf16[80,160]{1,0:T(8,128)(2,1)}, bf16[80,160]{1,0:T(8,128)(2,1)S(1)}, u32[]{:S(2)}, u32[]{:S(2)}) collective-permute-start(bf16[80,160]{1,0:T(8,128)(2,1)} %param.4), channel_id=1, source_target_pairs={{0,7},{1,6},{2,5},{3,4},{4,3},{5,2},{6,1},{7,0},{8,15},{9,14},{10,... | collective-permute-start | bytes 76808 | tf_op jit(solution)/shard_map/ppermute | solution.py:167
  4.5 0.8 %collective-permute-start.2 = (bf16[80,160]{1,0:T(8,128)(2,1)}, bf16[80,160]{1,0:T(8,128)(2,1)S(1)}, u32[]{:S(2)}, u32[]{:S(2)}) collective-permute-start(bf16[80,160]{1,0:T(8,128)(2,1)} %param.4), channel_id=1, source_target_pairs={{0,6},{1,7},{2,4},{3,5},{4,2},{5,3},{6,0},{7,1},{8,14},{9,15},{10,... | collective-permute-start | bytes 76808 | tf_op jit(solution)/shard_map/ppermute | solution.py:167
  5.6 0.1 compare_convert_fusion.pick
  5.9 0.6 %copy-done = s32[5,5]{1,0:T(8,128)S(1)} copy-done((s32[5,5]{1,0:T(8,128)S(1)}, s32[5,5]{1,0:T(8,128)}, u32[]{:S(2)}) %copy-start) | copy-done | bytes 124
  6.5 0.3 %fusion.3.refs_4_ = bf16[80,640]{1,0:T(8,128)(2,1)S(1)} fusion(s32[80]{0:T(128)S(1)} %and_select_fusion.3, s32[640]{0:T(1024)S(1)} %add_select_fusion, s32[5,5]{1,0:T(8,128)S(1)} %copy-done), kind=kOutput, calls=%fused_computation.2 | convolution fusion | flops 519625 | bytes 105380 | tf_op jit(solution)/shard_map/dot_general | solution.py:21
  6.9 1.3 %collective-permute-done.1.refs_1_ = bf16[80,160]{1,0:T(8,128)(2,1)S(1)} collective-permute-done((bf16[80,160]{1,0:T(8,128)(2,1)}, bf16[80,160]{1,0:T(8,128)(2,1)S(1)}, u32[]{:S(2)}, u32[]{:S(2)}) %collective-permute-start.1) | collective-permute-done | bytes 25632 | tf_op jit(solution)/shard_map/ppermute | solution.py:167
  8.2 1.0 %collective-permute-done.2.refs_2_ = bf16[80,160]{1,0:T(8,128)(2,1)S(1)} collective-permute-done((bf16[80,160]{1,0:T(8,128)(2,1)}, bf16[80,160]{1,0:T(8,128)(2,1)S(1)}, u32[]{:S(2)}, u32[]{:S(2)}) %collective-permute-start.2) | collective-permute-done | bytes 25632 | tf_op jit(solution)/shard_map/ppermute | solution.py:167
  9.2 0.2 shard_map.46
  9.4 0.6 %collective-permute-start.4 = (bf16[80,640]{1,0:T(8,128)(2,1)S(1)}, bf16[80,640]{1,0:T(8,128)(2,1)S(1)}, u32[]{:S(2)}, u32[]{:S(2)}) collective-permute-start(bf16[80,640]{1,0:T(8,128)(2,1)S(1)} %get-tuple-element.19.panel), channel_id=1, source_target_pairs={{0,4},{1,5},{2,6},{3,7},{4,0},{5,1},{6,2},{7,3},{8,12},{9,13},{10,... | collective-permute-start | bytes 307208 | tf_op jit(solution)/shard_map/ppermute | solution.py:167
  10.0 2.1 %collective-permute-start.5 = (bf16[80,480]{1,0:T(8,128)(2,1)S(1)}, bf16[80,480]{1,0:T(8,128)(2,1)S(1)}, u32[]{:S(2)}, u32[]{:S(2)}) collective-permute-start(bf16[80,480]{1,0:T(8,128)(2,1)S(1)} %get-tuple-element.26), channel_id=1, source_target_pairs={{0,28},{1,29},{2,30},{3,31},{4,24},{5,25},{6,26},{7,27},{8,20},{9,... | collective-permute-start | bytes 230408 | tf_op jit(solution)/shard_map/ppermute | solution.py:167
  12.1 0.5 %collective-permute-start.6 = (bf16[80,480]{1,0:T(8,128)(2,1)S(1)}, bf16[80,480]{1,0:T(8,128)(2,1)S(1)}, u32[]{:S(2)}, u32[]{:S(2)}) collective-permute-start(bf16[80,480]{1,0:T(8,128)(2,1)S(1)} %get-tuple-element.27), channel_id=1, source_target_pairs={{0,20},{1,21},{2,22},{3,23},{4,16},{5,17},{6,18},{7,19},{8,28},{9,... | collective-permute-start | bytes 230408 | tf_op jit(solution)/shard_map/ppermute | solution.py:167
  12.7 0.2 %collective-permute-start.7 = (bf16[80,480]{1,0:T(8,128)(2,1)S(1)}, bf16[80,480]{1,0:T(8,128)(2,1)S(1)}, u32[]{:S(2)}, u32[]{:S(2)}) collective-permute-start(bf16[80,480]{1,0:T(8,128)(2,1)S(1)} %get-tuple-element.28), channel_id=1, source_target_pairs={{0,12},{1,13},{2,14},{3,15},{4,8},{5,9},{6,10},{7,11},{8,4},{9,5},... | collective-permute-start | bytes 230408 | tf_op jit(solution)/shard_map/ppermute | solution.py:167
  12.9 0.2 %fusion.6 = bf16[160,5]{0,1:T(8,128)(2,1)S(1)} fusion(s32[160]{0:T(256)S(1)} %get-tuple-element.36, s32[5,5]{1,0:T(8,128)S(1)} %copy-done.2), kind=kOutput, calls=%fused_computation.6 | convolution fusion | flops 8825 | bytes 2340 | tf_op jit(solution)/shard_map/dot_general | solution.py:20
  13.1 0.5 %copy-done.1 = s32[5,5]{1,0:T(8,128)S(1)} copy-done((s32[5,5]{1,0:T(8,128)S(1)}, s32[5,5]{1,0:T(8,128)}, u32[]{:S(2)}) %copy-start.1) | copy-done | bytes 124
  13.6 0.3 %fusion.cube_keep = bf16[160,160]{1,0:T(8,128)(2,1)S(1)} fusion(s32[160]{0:T(256)S(1)} %get-tuple-element.36, s32[160]{0:T(256)S(1)} %get-tuple-element.35, s32[5,5]{1,0:T(8,128)S(1)} %copy-done.1), kind=kOutput, calls=%fused_computation | convolution fusion | flops 265625 | bytes 52580 | tf_op jit(solution)/shard_map/dot_general | solution.py:21
  13.9 0.2 %fusion.13.keep = bf16[160,240]{1,0:T(8,128)(2,1)S(1)} fusion(bf16[160,5]{0,1:T(8,128)(2,1)S(1)} %fusion.6, s32[240]{0:T(256)S(1)} %get-tuple-element.31), kind=kOutput, calls=%fused_computation.16 | convolution fusion | flops 385200 | bytes 79360 | tf_op jit(solution)/shard_map/dot_general | solution.py:21
  14.2 0.2 %fusion.18.keep = bf16[160,80]{1,0:T(8,128)(2,1)S(1)} fusion(bf16[160,5]{0,1:T(8,128)(2,1)S(1)} %fusion.6, s32[80]{0:T(128)S(1)} %and_select_fusion.3), kind=kOutput, calls=%fused_computation.28 | convolution fusion | flops 128400 | bytes 27520 | tf_op jit(solution)/shard_map/dot_general | solution.py:21
  14.4 0.7 %shard_map.47 = (f32[160,160]{1,0:T(8,128)S(1)}, bf16[160,480]{1,0:T(8,128)(2,1)S(1)}, f32[160,240]{1,0:T(8,128)S(1)}, bf16[240,160]{1,0:T(8,128)(2,1)S(1)}) custom-call(bf16[80,640]{1,0:T(8,128)(2,1)S(1)} %get-tuple-element.19.panel, bf16[80,640]{1,0:T(8,128)(2,1)S(1)} %collective-permute-done.4.other, bf16[160,80]{1,0:T(8,128)(2,1)S(1)} %fusion.18.keep, ...), custom_call_target="tpu_custom_call" | custom-call | tf_op jit(solution)/shard_map/pallas_call | solution.py:46
  15.1 0.3 %collective-permute-done.5.refs_0_ = bf16[80,480]{1,0:T(8,128)(2,1)S(1)} collective-permute-done((bf16[80,480]{1,0:T(8,128)(2,1)S(1)}, bf16[80,480]{1,0:T(8,128)(2,1)S(1)}, u32[]{:S(2)}, u32[]{:S(2)}) %collective-permute-start.5) | collective-permute-done | bytes 76832 | tf_op jit(solution)/shard_map/ppermute | solution.py:167
  15.4 1.9 %collective-permute-done.6.refs_1_ = bf16[80,480]{1,0:T(8,128)(2,1)S(1)} collective-permute-done((bf16[80,480]{1,0:T(8,128)(2,1)S(1)}, bf16[80,480]{1,0:T(8,128)(2,1)S(1)}, u32[]{:S(2)}, u32[]{:S(2)}) %collective-permute-start.6) | collective-permute-done | bytes 76832 | tf_op jit(solution)/shard_map/ppermute | solution.py:167
  17.3 0.4 %shard_map.48 = (f32[80,160]{1,0:T(8,128)S(1)}, f32[80,160]{1,0:T(8,128)S(1)}) custom-call(f32[160,160]{1,0:T(8,128)S(1)} %get-tuple-element.22.part, bf16[160,480]{1,0:T(8,128)(2,1)S(1)} %get-tuple-element.23.left, f32[160,240]{1,0:T(8,128)S(1)} %get-tuple-element.24.total, bf16[240,160]{1,0:T(8,128)(2,1)S(1)} %get-tuple-element.25.known, ...), custom_call_target="tpu_custom_call" | custom-call | tf_op jit(solution)/shard_map/pallas_call | solution.py:46
  17.8 0.2 collective-permute-start.8
  17.9 1.2 %collective-permute-done.8.b = f32[80,160]{1,0:T(8,128)S(1)} collective-permute-done((f32[80,160]{1,0:T(8,128)S(1)}, f32[80,160]{1,0:T(8,128)S(1)}, u32[]{:S(2)}, u32[]{:S(2)}) %collective-permute-start.8) | collective-permute-done | bytes 51232 | tf_op jit(solution)/shard_map/ppermute | solution.py:167
  19.1 0.7 %add.222 = f32[80,160]{1,0:T(8,128)} custom-call(f32[80,160]{1,0:T(8,128)S(1)} %get-tuple-element.29.a, f32[80,160]{1,0:T(8,128)S(1)} %collective-permute-done.8.b), custom_call_target="tpu_custom_call" | custom-call | tf_op jit(solution)/shard_map/add/pallas_call | solution.py:148
  (22 shorter events, 0.4 us)
Async XLA Ops:
  0.0 6.9 %collective-permute-start = (bf16[80,160]{1,0:T(8,128)(2,1)}, bf16[80,160]{1,0:T(8,128)(2,1)S(1)}, u32[]{:S(2)}, u32[]{:S(2)}) collective-permute-start(bf16[80,160]{1,0:T(8,128)(2,1)} %param.4), channel_id=1, source_target_pairs={{0,7},{1,6},{2,5},{3,4},{4,3},{5,2},{6,1},{7,0},{8,15},{9,14},{10,... | collective-permute-start | bytes 76808 | tf_op jit(solution)/shard_map/ppermute | solution.py:167
  4.5 3.6 %collective-permute-start.1 = (bf16[80,160]{1,0:T(8,128)(2,1)}, bf16[80,160]{1,0:T(8,128)(2,1)S(1)}, u32[]{:S(2)}, u32[]{:S(2)}) collective-permute-start(bf16[80,160]{1,0:T(8,128)(2,1)} %param.4), channel_id=1, source_target_pairs={{0,5},{1,4},{2,7},{3,6},{4,1},{5,0},{6,3},{7,2},{8,13},{9,12},{10,... | collective-permute-start | bytes 76808 | tf_op jit(solution)/shard_map/ppermute | solution.py:167
  4.5 4.6 %collective-permute-start.2 = (bf16[80,160]{1,0:T(8,128)(2,1)}, bf16[80,160]{1,0:T(8,128)(2,1)S(1)}, u32[]{:S(2)}, u32[]{:S(2)}) collective-permute-start(bf16[80,160]{1,0:T(8,128)(2,1)} %param.4), channel_id=1, source_target_pairs={{0,6},{1,7},{2,4},{3,5},{4,2},{5,3},{6,0},{7,1},{8,14},{9,15},{10,... | collective-permute-start | bytes 76808 | tf_op jit(solution)/shard_map/ppermute | solution.py:167
  5.4 3.8 %collective-permute-start.3 = (bf16[80,160]{1,0:T(8,128)(2,1)}, bf16[80,160]{1,0:T(8,128)(2,1)S(1)}, u32[]{:S(2)}, u32[]{:S(2)}) collective-permute-start(bf16[80,160]{1,0:T(8,128)(2,1)} %param.4), channel_id=1, source_target_pairs={{0,4},{1,5},{2,6},{3,7},{4,0},{5,1},{6,2},{7,3},{8,12},{9,13},{10,... | collective-permute-start | bytes 76808 | tf_op jit(solution)/shard_map/ppermute | solution.py:167
  5.8 0.7 %copy-start = (s32[5,5]{1,0:T(8,128)S(1)}, s32[5,5]{1,0:T(8,128)}, u32[]{:S(2)}) copy-start(s32[5,5]{1,0:T(8,128)} %param.5) | copy-start | bytes 304
  9.4 3.5 %copy-start.2 = (s32[5,5]{1,0:T(8,128)S(1)}, s32[5,5]{1,0:T(8,128)}, u32[]{:S(2)}) copy-start(s32[5,5]{1,0:T(8,128)} %param.6) | copy-start | bytes 304
  9.4 5.0 %collective-permute-start.4 = (bf16[80,640]{1,0:T(8,128)(2,1)S(1)}, bf16[80,640]{1,0:T(8,128)(2,1)S(1)}, u32[]{:S(2)}, u32[]{:S(2)}) collective-permute-start(bf16[80,640]{1,0:T(8,128)(2,1)S(1)} %get-tuple-element.19.panel), channel_id=1, source_target_pairs={{0,4},{1,5},{2,6},{3,7},{4,0},{5,1},{6,2},{7,3},{8,12},{9,13},{10,... | collective-permute-start | bytes 307208 | tf_op jit(solution)/shard_map/ppermute | solution.py:167
  10.0 5.4 %collective-permute-start.5 = (bf16[80,480]{1,0:T(8,128)(2,1)S(1)}, bf16[80,480]{1,0:T(8,128)(2,1)S(1)}, u32[]{:S(2)}, u32[]{:S(2)}) collective-permute-start(bf16[80,480]{1,0:T(8,128)(2,1)S(1)} %get-tuple-element.26), channel_id=1, source_target_pairs={{0,28},{1,29},{2,30},{3,31},{4,24},{5,25},{6,26},{7,27},{8,20},{9,... | collective-permute-start | bytes 230408 | tf_op jit(solution)/shard_map/ppermute | solution.py:167
  12.1 5.2 %collective-permute-start.6 = (bf16[80,480]{1,0:T(8,128)(2,1)S(1)}, bf16[80,480]{1,0:T(8,128)(2,1)S(1)}, u32[]{:S(2)}, u32[]{:S(2)}) collective-permute-start(bf16[80,480]{1,0:T(8,128)(2,1)S(1)} %get-tuple-element.27), channel_id=1, source_target_pairs={{0,20},{1,21},{2,22},{3,23},{4,16},{5,17},{6,18},{7,19},{8,28},{9,... | collective-permute-start | bytes 230408 | tf_op jit(solution)/shard_map/ppermute | solution.py:167
  12.7 4.6 %collective-permute-start.7 = (bf16[80,480]{1,0:T(8,128)(2,1)S(1)}, bf16[80,480]{1,0:T(8,128)(2,1)S(1)}, u32[]{:S(2)}, u32[]{:S(2)}) collective-permute-start(bf16[80,480]{1,0:T(8,128)(2,1)S(1)} %get-tuple-element.28), channel_id=1, source_target_pairs={{0,12},{1,13},{2,14},{3,15},{4,8},{5,9},{6,10},{7,11},{8,4},{9,5},... | collective-permute-start | bytes 230408 | tf_op jit(solution)/shard_map/ppermute | solution.py:167
  12.9 0.7 %copy-start.1 = (s32[5,5]{1,0:T(8,128)S(1)}, s32[5,5]{1,0:T(8,128)}, u32[]{:S(2)}) copy-start(s32[5,5]{1,0:T(8,128)} %param.7) | copy-start | bytes 304
  17.8 1.3 %collective-permute-start.8 = (f32[80,160]{1,0:T(8,128)S(1)}, f32[80,160]{1,0:T(8,128)S(1)}, u32[]{:S(2)}, u32[]{:S(2)}) collective-permute-start(f32[80,160]{1,0:T(8,128)S(1)} %get-tuple-element.30), channel_id=1, source_target_pairs={{0,4},{1,5},{2,6},{3,7},{4,0},{5,1},{6,2},{7,3},{8,12},{9,13},{10,... | collective-permute-start | bytes 153608 | tf_op jit(solution)/shard_map/ppermute | solution.py:167
